TPU v7x, 32 devices: a 4x4x1 block of a 4x4x8 slice. The times are simulated.
32 devices in a mesh: dp: 1 (over z), cp: 32 (over y, x, core).
Axes of the slice: x: 4, y: 4, z: 1, core: 2. Of those that a mesh axis runs over, the one named last changes fastest.
The devices are a block of a 4x4x8 slice.
Arguments:
- hidden: bfloat16 [1, 8192, 2560], P('dp', 'cp')
- grad_out: bfloat16 [1, 8192, 2560], P('dp', 'cp')
- norm_gain: float32 [2, 2560], replicated
- w_qkv: bfloat16 [2, 2560, 4096], replicated
- b_qkv: float32 [2, 4096], replicated
- w_out: bfloat16 [2, 2048, 2560], replicated
- b_out: float32 [2, 2560], replicated
- attn_sinks: float32 [2, 8], replicated
Outputs:
- output 1: bfloat16 [1, 8192, 2560], P('dp', 'cp')
- output 2: bfloat16 [1, 8192, 2560], P('dp', 'cp')
- output 3: float32 [32, 2, 2560], P(('dp', 'cp'))
- output 4: float32 [32, 2, 4096], P(('dp', 'cp'))
- output 5: float32 [32, 2, 2560], P(('dp', 'cp'))
- output 6: float32 [32, 2, 8], P(('dp', 'cp'))
All inputs are finite; a program needn't handle non-finite values.
Results may differ from a plain program's by a relative error of at most 0.0170665.
Values are sent between devices in bfloat16 or wider.
A program may use at most 768 MiB of HBM per device.

v0:
```python
import jax
import jax.numpy as jnp
import math
from jax import lax
from jax.sharding import PartitionSpec as P

WINDOW = 128
EPSILON = 1e-5
ROPE_THETA = 150000.0
YARN_FACTOR = 32.0
YARN_CONTEXT = 4096.0
YARN_ALPHA = 1.0
YARN_BETA = 32.0


def rope_tables(positions, head_dim):
    half_dim = head_dim // 2
    freq_steps = jnp.arange(half_dim, dtype=jnp.float32)
    freq_base = ROPE_THETA ** (freq_steps * 2.0 / head_dim)
    concentration = 0.1 * math.log(YARN_FACTOR) + 1.0
    low_edge = half_dim * math.log(YARN_CONTEXT / (YARN_BETA * 2.0 * math.pi)) / math.log(ROPE_THETA)
    high_edge = half_dim * math.log(YARN_CONTEXT / (YARN_ALPHA * 2.0 * math.pi)) / math.log(ROPE_THETA)
    ramp_pos = jnp.clip((freq_steps - low_edge) / (high_edge - low_edge), 0.0, 1.0)
    inv_freq = (1.0 - ramp_pos) / freq_base + ramp_pos / (YARN_FACTOR * freq_base)
    angles = positions.astype(jnp.float32)[:, None] * inv_freq[None, :]
    return jnp.cos(angles) * concentration, jnp.sin(angles) * concentration


def rotate_half(tensor, cos_tab, sin_tab):
    half_dim = tensor.shape[-1] // 2
    first_half = tensor[..., :half_dim]
    second_half = tensor[..., half_dim:]
    return jnp.concatenate([first_half * cos_tab - second_half * sin_tab, second_half * cos_tab + first_half * sin_tab], axis=-1)


def norm_project(hid_f, gain_row, w_in, bias_row, cos_tab, sin_tab, num_heads, kv_heads):
    batch_size, seq_dev = hid_f.shape[0], hid_f.shape[1]
    head_dim = 2 * cos_tab.shape[-1]
    q_width = num_heads * head_dim
    k_width = kv_heads * head_dim
    inv_rms = lax.rsqrt(jnp.mean(hid_f * hid_f, axis=-1, keepdims=True) + EPSILON)
    normed = (hid_f * inv_rms * gain_row).astype(jnp.bfloat16)
    projected = jnp.dot(normed, w_in, preferred_element_type=jnp.float32) + bias_row
    query_rows = rotate_half(projected[..., :q_width].reshape(batch_size, seq_dev, kv_heads, num_heads // kv_heads, head_dim), cos_tab[:, None, None, :], sin_tab[:, None, None, :])
    key_rows = rotate_half(projected[..., q_width:q_width + k_width].reshape(batch_size, seq_dev, kv_heads, head_dim), cos_tab[:, None, :], sin_tab[:, None, :])
    value_rows = projected[..., q_width + k_width:].reshape(batch_size, seq_dev, kv_heads, head_dim)
    return query_rows.astype(jnp.bfloat16), key_rows.astype(jnp.bfloat16), value_rows.astype(jnp.bfloat16), inv_rms


def attend_forward(query_rows, key_rows, value_rows, sink_row, row_pos, key_pos, window_on, logit_scale):
    kv_heads, group_size = query_rows.shape[2], query_rows.shape[3]
    scores = jnp.einsum('bqkgd,bskd->bkgqs', query_rows, key_rows, preferred_element_type=jnp.float32) * logit_scale
    key_mask = (key_pos[None, :] <= row_pos[:, None]) & (key_pos[None, :] >= 0)
    if window_on:
        key_mask = key_mask & (key_pos[None, :] >= row_pos[:, None] - WINDOW)
    scores = jnp.where(key_mask, scores, -jnp.inf)
    sink_grid = sink_row.reshape(kv_heads, group_size)[None, :, :, None]
    row_peak = jnp.maximum(jnp.max(scores, axis=-1), sink_grid)
    exp_scores = jnp.exp(scores - row_peak[..., None])
    sink_exp = jnp.exp(sink_grid - row_peak)
    denominator = jnp.sum(exp_scores, axis=-1) + sink_exp
    prob_f32 = exp_scores / denominator[..., None]
    prob_bf = prob_f32.astype(jnp.bfloat16)
    attn_out = jnp.einsum('bkgqs,bskd->bqkgd', prob_bf, value_rows, preferred_element_type=jnp.float32).astype(jnp.bfloat16)
    return attn_out, prob_f32, prob_bf, sink_exp / denominator


def attend_backward(d_attn, query_rows, key_rows, value_rows, prob_f32, prob_bf, sink_prob, logit_scale):
    d_prob = jnp.einsum('bqkgd,bskd->bkgqs', d_attn, value_rows, preferred_element_type=jnp.float32).astype(jnp.bfloat16).astype(jnp.float32)
    row_delta = jnp.sum(prob_f32 * d_prob, axis=-1)
    d_scores = (prob_f32 * (d_prob - row_delta[..., None])).astype(jnp.bfloat16)
    d_query = (jnp.einsum('bkgqs,bskd->bqkgd', d_scores, key_rows, preferred_element_type=jnp.float32) * logit_scale).astype(jnp.bfloat16)
    d_keys = jnp.einsum('bkgqs,bqkgd->bskd', d_scores, query_rows, preferred_element_type=jnp.float32) * logit_scale
    d_values = jnp.einsum('bkgqs,bqkgd->bskd', prob_bf, d_attn, preferred_element_type=jnp.float32)
    d_sink = -jnp.sum(sink_prob * row_delta, axis=(0, 3)).reshape(-1)
    return d_query, d_keys, d_values, d_sink


def project_backward(d_query, d_keys, d_values, hid_f, inv_rms, gain_row, w_in, cos_tab, sin_tab):
    batch_size, seq_dev = hid_f.shape[0], hid_f.shape[1]
    dq_rot = rotate_half(d_query.astype(jnp.float32), cos_tab[:, None, None, :], -sin_tab[:, None, None, :]).reshape(batch_size, seq_dev, -1)
    dk_rot = rotate_half(d_keys.astype(jnp.float32), cos_tab[:, None, :], -sin_tab[:, None, :]).reshape(batch_size, seq_dev, -1)
    d_proj = jnp.concatenate([dq_rot, dk_rot, d_values.astype(jnp.float32).reshape(batch_size, seq_dev, -1)], axis=-1)
    d_bias = jnp.sum(d_proj, axis=(0, 1))
    d_normed = jnp.einsum('bsq,dq->bsd', d_proj.astype(jnp.bfloat16), w_in, preferred_element_type=jnp.float32).astype(jnp.bfloat16).astype(jnp.float32)
    d_gain = jnp.sum(d_normed * hid_f * inv_rms, axis=(0, 1))
    unit_grad = d_normed * gain_row
    d_hid = inv_rms * unit_grad - hid_f * inv_rms ** 3 * jnp.mean(unit_grad * hid_f, axis=-1, keepdims=True)
    return d_hid, d_gain, d_bias


def dense_out(attn_out, w_proj, bias_row):
    batch_size, seq_dev = attn_out.shape[0], attn_out.shape[1]
    return jnp.dot(attn_out.reshape(batch_size, seq_dev, -1), w_proj, preferred_element_type=jnp.float32) + bias_row


def solution(mesh):
    num_shards = mesh.shape['cp']
    forward_pairs = [(source, source + 1) for source in range(num_shards - 1)]
    backward_pairs = [(source + 1, source) for source in range(num_shards - 1)]
    row_spec = P('dp', 'cp')
    device_spec = P(('dp', 'cp'))
    whole_spec = P()

    def local_step(hidden, grad_out, norm_gain, w_qkv, b_qkv, w_out, b_out, attn_sinks):
        seq_dev = hidden.shape[1]
        num_heads = attn_sinks.shape[1]
        head_dim = w_out.shape[1] // num_heads
        kv_heads = (w_qkv.shape[2] // head_dim - num_heads) // 2
        logit_scale = head_dim ** -0.5
        shard_start = lax.axis_index('cp') * seq_dev
        row_pos = shard_start + jnp.arange(seq_dev)
        cos_tab, sin_tab = rope_tables(row_pos, head_dim)

        hid_one = hidden.astype(jnp.float32)
        query_one, keys_one, values_one, rms_one = norm_project(hid_one, norm_gain[0], w_qkv[0], b_qkv[0], cos_tab, sin_tab, num_heads, kv_heads)
        tail_rows = jnp.concatenate([keys_one[:, seq_dev - WINDOW:], values_one[:, seq_dev - WINDOW:]], axis=2)
        prev_rows = lax.ppermute(tail_rows, 'cp', forward_pairs)
        near_keys = jnp.concatenate([prev_rows[:, :, :kv_heads], keys_one], axis=1)
        near_values = jnp.concatenate([prev_rows[:, :, kv_heads:], values_one], axis=1)
        near_pos = jnp.concatenate([shard_start - WINDOW + jnp.arange(WINDOW), row_pos])
        attn_one, prob_one, probbf_one, sink_one = attend_forward(query_one, near_keys, near_values, attn_sinks[0], row_pos, near_pos, True, logit_scale)
        middle = (hid_one + dense_out(attn_one, w_out[0], b_out[0])).astype(jnp.bfloat16)

        hid_two = middle.astype(jnp.float32)
        query_two, keys_two, values_two, rms_two = norm_project(hid_two, norm_gain[1], w_qkv[1], b_qkv[1], cos_tab, sin_tab, num_heads, kv_heads)
        all_rows = lax.all_gather(jnp.concatenate([keys_two, values_two], axis=2), 'cp', axis=1, tiled=True)
        far_keys = all_rows[:, :, :kv_heads]
        far_values = all_rows[:, :, kv_heads:]
        far_pos = jnp.arange(all_rows.shape[1])
        attn_two, prob_two, probbf_two, sink_two = attend_forward(query_two, far_keys, far_values, attn_sinks[1], row_pos, far_pos, False, logit_scale)
        output = (hid_two + dense_out(attn_two, w_out[1], b_out[1])).astype(jnp.bfloat16)

        d_out_two = grad_out.astype(jnp.float32)
        d_attn_two = jnp.einsum('bsd,qd->bsq', grad_out, w_out[1], preferred_element_type=jnp.float32).astype(jnp.bfloat16).reshape(query_two.shape)
        dq_two, dk_far, dv_far, dsink_two = attend_backward(d_attn_two, query_two, far_keys, far_values, prob_two, probbf_two, sink_two, logit_scale)
        own_two = lax.psum_scatter(jnp.concatenate([dk_far, dv_far], axis=2).astype(jnp.bfloat16), 'cp', scatter_dimension=1, tiled=True)
        dhid_two, dgain_two, dbias_two = project_backward(dq_two, own_two[:, :, :kv_heads], own_two[:, :, kv_heads:], hid_two, rms_two, norm_gain[1], w_qkv[1], cos_tab, sin_tab)
        d_middle = (d_out_two + dhid_two).astype(jnp.bfloat16)

        d_mid_f = d_middle.astype(jnp.float32)
        d_attn_one = jnp.einsum('bsd,qd->bsq', d_middle, w_out[0], preferred_element_type=jnp.float32).astype(jnp.bfloat16).reshape(query_one.shape)
        dq_one, dk_near, dv_near, dsink_one = attend_backward(d_attn_one, query_one, near_keys, near_values, prob_one, probbf_one, sink_one, logit_scale)
        near_grad = jnp.concatenate([dk_near, dv_near], axis=2)
        prev_grad = lax.ppermute(near_grad[:, :WINDOW].astype(jnp.bfloat16), 'cp', backward_pairs)
        own_grad = near_grad[:, WINDOW:]
        cut_row = seq_dev - WINDOW
        own_one = jnp.concatenate([own_grad[:, :cut_row], own_grad[:, cut_row:] + prev_grad.astype(jnp.float32)], axis=1).astype(jnp.bfloat16)
        dhid_one, dgain_one, dbias_one = project_backward(dq_one, own_one[:, :, :kv_heads], own_one[:, :, kv_heads:], hid_one, rms_one, norm_gain[0], w_qkv[0], cos_tab, sin_tab)
        d_hidden = (d_mid_f + dhid_one).astype(jnp.bfloat16)

        d_gain = jnp.stack([dgain_one, dgain_two])[None]
        d_bias_qkv = jnp.stack([dbias_one, dbias_two])[None]
        d_bias_out = jnp.stack([jnp.sum(d_mid_f, axis=(0, 1)), jnp.sum(d_out_two, axis=(0, 1))])[None]
        d_sinks = jnp.stack([dsink_one, dsink_two])[None]
        return output, d_hidden, d_gain, d_bias_qkv, d_bias_out, d_sinks

    return jax.shard_map(local_step, mesh=mesh, in_specs=(row_spec, row_spec, whole_spec, whole_spec, whole_spec, whole_spec, whole_spec, whole_spec), out_specs=(row_spec, row_spec, device_spec, device_spec, device_spec, device_spec), check_vma=False)
```

profile of v0, /device:TPU:97, one launch (start us, length us, event | category | flops | bytes accessed | tf_op | source)
XLA Modules:
  0.0 661.7 jit_solution(5303342367540707503)
XLA Ops:
  11.8 10.3 %fusion.48 = f32[1,256,4096]{2,1,0:T(8,128)S(1)} fusion(bf16[2,2560,4096]{2,1,0:T(8,128)(2,1)} %param.11, f32[4096]{0:T(1024)S(1)} %bitcast.395, bf16[1,256,2560]{2,1,0:T(8,128)(2,1)} %param.8, f32[2560]{0:T(1024)S(1)} %get-tuple-element.13, f32[256]{0:T(256)S(1)} %get-tuple-element.58), kind=kOutput, calls=%fused_computation.66 | convolution fusion | flops 5372379136 | bytes 26504192 | tf_op jit(solution)/shard_map/dot_general | solution.py:43
  22.3 1.9 copy-done.7
  30.2 4.8 collective-permute-start
  36.1 2.8 reshape.818
  38.9 2.3 fusion.208
  43.9 1.8 fusion.123
  47.5 1.8 copy.48
  49.3 2.3 fusion.140
  51.6 7.2 %fusion.109 = (f32[256]{0:T(256)S(1)}, bf16[1,256,2560]{2,1,0:T(8,128)(2,1)S(1)}) fusion(f32[2560]{0:T(1024)S(1)} %get-tuple-element.11, bf16[256,2048]{0,1:T(8,128)(2,1)S(1)} %bitcast.397, bf16[2,2048,2560]{2,1,0:T(8,128)(2,1)} %param.13, bf16[1,256,2560]{2,1,0:T(8,128)(2,1)S(1)} %copy-done.9), kind=kOutput, calls=%fused_computation.109 | convolution fusion | flops 2688941824 | bytes 14167040 | tf_op jit(solution)/shard_map/dot_general | solution.py:94
  59.5 10.0 %fusion.54 = f32[1,256,4096]{2,1,0:T(8,128)S(1)} fusion(bf16[2,2560,4096]{2,1,0:T(8,128)(2,1)} %param.11, f32[4096]{0:T(1024)S(1)} %bitcast.394, bf16[1,256,2560]{2,1,0:T(8,128)(2,1)S(1)} %get-tuple-element.64, f32[2560]{0:T(1024)S(1)} %get-tuple-element.12, f32[256]{0:T(256)S(1)} %get-tuple-element.60), kind=kOutput, calls=%fused_computation.68 | convolution fusion | flops 5372379136 | bytes 26504192 | tf_op jit(solution)/shard_map/dot_general | solution.py:43
  69.5 1.9 copy-done.20
  74.4 6.9 %fusion.120 = bf16[256,2048]{1,0:T(8,128)(2,1)S(1)} fusion(bf16[2,2048,2560]{2,1,0:T(8,128)(2,1)} %param.13, bf16[1,256,2560]{2,1,0:T(8,128)(2,1)S(1)} %copy-done.27), kind=kOutput, calls=%fused_computation.118 | convolution fusion | flops 2684878848 | bytes 12845056 | tf_op jit(solution)/shard_map/bsd,qd->bsq/dot_general | solution.py:135
  84.0 3.2 slice.217
  87.2 2.9 copy.58
  90.1 3.1 fusion.207
  94.7 2.6 copy.140
  97.3 2.5 fusion.168
  99.8 85.3 %all-gather.2.cloned.1.call-done = bf16[1,8192,8,256]{3,1,2,0:T(8,128)(2,1)} async-done(((bf16[1,256,8,256]{3,1,2,0:T(8,128)(2,1)}), bf16[1,8192,8,256]{3,1,2,0:T(8,128)(2,1)}) %all-gather.2.cloned.1.call-update) | async-done | bytes 33554448 | tf_op jit(solution)/shard_map/all_gather | solution.py:127
  185.1 29.2 %fusion.7 = (f32[4,2,256]{2,1,0:T(2,128)S(1)}, f32[4,8192,256,2]{2,1,3,0:T(8,128)}) fusion(pred[256,8192]{0,1:T(8,128)(4,1)S(1)} %iota_compare_fusion, bf16[256,4,2,128]{3,0,2,1:T(8,128)(2,1)} %get-tuple-element.23, bf16[256,4,2,128]{3,0,2,1:T(8,128)(2,1)} %get-tuple-element.22, bf16[1,8192,8,256]{3,1,2,0:T(8,128)(2,1)} %all-gather.2.cloned.1.call-done), kind=kOutput, calls=%fused_computation.10 | convolution fusion | flops 8642361344 | bytes 87040000 | tf_op jit(solution)/shard_map/bqkgd,bskd->bkgqs/dot_general | solution.py:52
  214.4 21.6 %fusion.6 = f32[4,2,256]{2,1,0:T(2,128)S(1)} fusion(f32[4,8192,256,2]{2,1,3,0:T(8,128)} %get-tuple-element.66, f32[4,2,256]{2,1,0:T(2,128)S(1)} %broadcast_maximum_fusion, pred[256,8192]{0,1:T(8,128)(4,1)S(1)} %iota_compare_fusion), kind=kLoop, calls=%fused_computation.9 | loop fusion | flops 67106816 | bytes 69222400 | tf_op jit(solution)/shard_map/reduce_sum | solution.py:61
  236.2 32.1 %fusion.27 = bf16[1,8192,4,256]{3,1,2,0:T(8,128)(2,1)} fusion(bf16[256,4,2,256]{0,3,2,1:T(8,128)(2,1)S(1)} %bitcast.384, f32[4,2,256]{2,1,0:T(2,128)S(1)} %fusion.177, f32[4,2,256]{2,1,0:T(2,128)S(1)} %broadcast_maximum_fusion, f32[4,8192,256,2]{2,1,3,0:T(8,128)} %get-tuple-element.66, pred[256,8192]{0,1:T(8,128)(4,1)S(1)} %iota_compare_fusion), kind=kOutput, calls=%fused_computation.34 | convolution fusion | flops 8682209280 | bytes 87048192 | tf_op jit(solution)/shard_map/bkgqs,bqkgd->bskd/dot_general | solution.py:74
  268.2 44.3 %fusion.2 = (f32[4,2,256]{2,1,0:T(2,128)S(1)}, bf16[4,8192,256,2]{2,1,3,0:T(8,128)(2,1)}) fusion(f32[4,2,256]{2,1,0:T(2,128)S(1)} %fusion.177, f32[4,2,256]{2,1,0:T(2,128)S(1)} %broadcast_maximum_fusion, f32[4,8192,256,2]{2,1,3,0:T(8,128)} %get-tuple-element.66, pred[256,8192]{0,1:T(8,128)(4,1)S(1)} %iota_compare_fusion, ...), kind=kOutput, calls=%fused_computation.4 | convolution fusion | flops 8724150272 | bytes 120610816 | tf_op jit(solution)/shard_map/bqkgd,bskd->bkgqs/dot_general | solution.py:69
  312.5 43.7 %fusion.8 = bf16[4,2,256,8192]{2,3,1,0:T(8,128)(2,1)} fusion(bf16[4,8192,256,2]{2,1,3,0:T(8,128)(2,1)} %get-tuple-element.68, f32[4,2,256]{2,1,0:T(2,128)S(1)} %get-tuple-element.67, f32[4,2,256]{2,1,0:T(2,128)S(1)} %fusion.177, f32[4,2,256]{2,1,0:T(2,128)S(1)} %broadcast_maximum_fusion, f32[4,8192,256,2]{2,1,3,0:T(8,128)} %get-tuple-element.66, ...), kind=kLoop, calls=%fused_computation.11 | loop fusion | flops 134217728 | bytes 136339456 | tf_op jit(solution)/shard_map/reshape.76
  356.2 30.3 %fusion.32 = bf16[1,8192,4,256]{3,1,2,0:T(8,128)(2,1)} fusion(bf16[4,2,256,8192]{2,3,1,0:T(8,128)(2,1)} %fusion.8, bf16[256,4,2,128]{3,0,2,1:T(8,128)(2,1)S(1)} %copy-done.38, bf16[256,4,2,128]{3,0,2,1:T(8,128)(2,1)S(1)} %copy-done.37), kind=kOutput, calls=%fused_computation.39 | convolution fusion | flops 8608808960 | bytes 51380224 | tf_op jit(solution)/shard_map/bkgqs,bqkgd->bskd/dot_general | solution.py:73
  386.5 22.9 %pad_maximum_fusion = bf16[1,8192,8,256]{3,1,2,0:T(8,128)(2,1)} fusion(bf16[1,8192,4,256]{3,1,2,0:T(8,128)(2,1)} %fusion.27, bf16[1,8192,4,256]{3,1,2,0:T(8,128)(2,1)} %fusion.32), kind=kLoop, calls=%fused_computation.12 | loop fusion | flops 16777216 | bytes 67108864 | tf_op jit(solution)/shard_map/concatenate | solution.py:137
  409.5 20.6 %convert_bitcast_fusion.3 = f32[1,256,4,2,256]{4,1,3,2,0:T(8,128)} fusion(bf16[4,2,256,8192]{2,3,1,0:T(8,128)(2,1)} %fusion.8, bf16[1,8192,8,256]{3,1,2,0:T(8,128)(2,1)} %all-gather.2.cloned.1.call-done), kind=kOutput, calls=%fused_computation.133 | convolution fusion | flops 8591507456 | bytes 52428800 | tf_op jit(solution)/shard_map/bkgqs,bskd->bqkgd/dot_general | solution.py:72
  430.1 1.8 multiply_subtract_fusion.1
  433.9 2.3 copy.67
  437.0 2.7 pad_maximum_fusion.2
  439.7 2.9 copy.93
  442.6 30.7 %fusion.146 = bf16[4,256,2,256]{3,1,2,0:T(8,128)(2,1)S(1)} fusion(bf16[1,8192,8,256]{3,1,2,0:T(8,128)(2,1)} %all-gather.2.cloned.1.call-done, f32[4,2,256]{2,1,0:T(2,128)S(1)} %fusion.177, f32[4,2,256]{2,1,0:T(2,128)S(1)} %broadcast_maximum_fusion, f32[4,8192,256,2]{2,1,3,0:T(8,128)} %get-tuple-element.66, pred[256,8192]{0,1:T(8,128)(4,1)S(1)} %iota_compare_fusion), kind=kOutput, calls=%fused_computation.146 | convolution fusion | flops 8674344960 | bytes 87048192 | tf_op jit(solution)/shard_map/bkgqs,bskd->bqkgd/dot_general | solution.py:64
  473.3 8.3 %fusion.76 = bf16[1,256,2560]{2,1,0:T(8,128)(2,1)} fusion(bf16[256,2048]{0,1:T(8,128)(2,1)S(1)} %bitcast.396, bf16[2,2048,2560]{2,1,0:T(8,128)(2,1)} %param.13, bf16[1,256,2560]{2,1,0:T(8,128)(2,1)} %copy-done.28, f32[2560]{0:T(1024)S(1)} %copy-done.63), kind=kOutput, calls=%fused_computation.76 | convolution fusion | flops 2686976000 | bytes 14166016 | tf_op jit(solution)/shard_map/dot_general | solution.py:94
  481.6 82.9 %reduce-scatter.2.cloned.1.call-done = bf16[1,256,8,256]{3,1,2,0:T(8,128)(2,1)} async-done(((bf16[1,8192,8,256]{3,1,2,0:T(8,128)(2,1)}), bf16[1,256,8,256]{3,1,2,0:T(8,128)(2,1)}) %reduce-scatter.2.cloned.1.call-update) | async-done | bytes 1048592 | tf_op jit(solution)/shard_map/reduce_scatter | solution.py:137
  564.6 2.4 slice_convert_fusion.3
  569.4 11.6 %fusion.116 = (f32[2560]{0:T(1024)}, f32[256]{0:T(256)S(1)}, f32[256,2560]{1,0:T(8,128)S(1)}) fusion(bf16[1,256,2560]{2,1,0:T(8,128)(2,1)} %copy-done.28, f32[256]{0:T(256)S(1)} %copy-done.70, f32[2560]{0:T(1024)S(1)} %copy-done.54, bf16[2,2560,4096]{2,1,0:T(8,128)(2,1)} %param.11, bf16[256,1024]{0,1:T(8,128)(2,1)} %bitcast.390, ...), kind=kOutput, calls=%fused_computation.116 | convolution fusion | flops 5380895744 | bytes 27023360 | tf_op jit(solution)/shard_map/bsq,dq->bsd/dot_general | solution.py:85
  580.9 3.2 convert_reduce_fusion
  585.2 8.1 %fusion.117 = bf16[256,2048]{1,0:T(8,128)(2,1)} fusion(bf16[2,2048,2560]{2,1,0:T(8,128)(2,1)} %param.13, bf16[1,256,2560]{2,1,0:T(8,128)(2,1)S(1)} %get-tuple-element.17), kind=kOutput, calls=%fused_computation.117 | convolution fusion | flops 2684878848 | bytes 12845056 | tf_op jit(solution)/shard_map/bsd,qd->bsq/dot_general | solution.py:142
  593.2 2.5 copy.142
  595.8 2.7 fusion.94
  603.2 2.1 fusion.143
  612.1 3.5 collective-permute-start.1
  616.2 3.2 copy.90
  619.4 2.6 copy.94
  623.3 2.4 copy.81
  625.7 2.8 maximum_reduce_fusion.1
  636.5 12.1 %fusion.108 = (f32[2560]{0:T(1024)S(1)}, f32[256]{0:T(256)S(1)}, f32[256,2560]{1,0:T(8,128)}) fusion(bf16[1,256,2560]{2,1,0:T(8,128)(2,1)S(1)} %copy-done.10, f32[256]{0:T(256)S(1)} %copy-done.67, f32[2560]{0:T(1024)S(1)} %copy-done.52, bf16[2,2560,4096]{2,1,0:T(8,128)(2,1)} %param.11, bf16[256,1024]{0,1:T(8,128)(2,1)} %bitcast.388, ...), kind=kOutput, calls=%fused_computation.108 | convolution fusion | flops 5380895744 | bytes 27023360 | tf_op jit(solution)/shard_map/bsq,dq->bsd/dot_general | solution.py:85
  648.6 2.3 maximum_reduce_fusion
  652.2 2.1 fusion.100
  (241 shorter events, 53.2 us)
Async XLA Ops:
  7.2 177.9 %all-gather.2.cloned.1.call-start = ((), (), s32[]{:S(2)}) async-start(), calls=%async_computation.1 | async-start | bytes 34603008 | tf_op jit(solution)/shard_map/all_gather | solution.py:127
  8.1 14.0 %copy-start.51 = (f32[2560]{0:T(1024)}, f32[2560]{0:T(1024)S(1)}, u32[]{:S(2)}) copy-start(f32[2560]{0:T(1024)S(1)} %get-tuple-element.13) | copy-start | bytes 30724
  8.1 51.3 %copy-start.53 = (f32[2560]{0:T(1024)}, f32[2560]{0:T(1024)S(1)}, u32[]{:S(2)}) copy-start(f32[2560]{0:T(1024)S(1)} %get-tuple-element.12) | copy-start | bytes 30724
  10.4 11.8 %copy-start.66 = (f32[256]{0:T(256)}, f32[256]{0:T(256)S(1)}, u32[]{:S(2)}) copy-start(f32[256]{0:T(256)S(1)} %get-tuple-element.58) | copy-start | bytes 3076
  28.5 68.8 %copy-start.3 = (f32[256,128]{1,0:T(8,128)}, f32[256,128]{1,0:T(8,128)S(1)}, u32[]{:S(2)}) copy-start(f32[256,128]{1,0:T(8,128)S(1)} %get-tuple-element.56) | copy-start | bytes 393220
  29.3 6.8 %slice-start = ((f32[1,256,4096]{2,1,0:T(8,128)}), f32[1,256,2048]{2,1,0:T(8,128)S(1)}, s32[]{:S(2)}) async-start(f32[1,256,4096]{2,1,0:T(8,128)} %copy-done.7), calls=%async_computation.3 | async-start | bytes 4194304 | tf_op jit(solution)/shard_map/slice | solution.py:44
  30.2 12.9 %collective-permute-start = (bf16[1,128,8,256]{3,1,2,0:T(8,128)(2,1)}, bf16[1,128,8,256]{3,1,2,0:T(8,128)(2,1)S(1)}, u32[]{:S(2)}, u32[]{:S(2)}) collective-permute-start(bf16[1,128,8,256]{3,1,2,0:T(8,128)(2,1)} %fusion.172), channel_id=1, source_target_pairs={{0,1},{1,2},{2,3},{3,4},{4,5},{5,6},{6,7},{7,8},{8,9},{9,10},{10,1... | collective-permute-start | bytes 1572872 | tf_op jit(solution)/shard_map/ppermute | solution.py:118
  38.9 2.9 copy-start.61
  41.8 4.7 copy-start.57
  42.6 6.6 %copy-start.35 = (pred[256,384]{0,1:T(8,128)(4,1)}, pred[256,384]{0,1:T(8,128)(4,1)S(1)}, u32[]{:S(2)}) copy-start(pred[256,384]{0,1:T(8,128)(4,1)S(1)} %compare_and_fusion) | copy-start | bytes 294916
  45.7 5.8 copy-start
  45.8 5.8 copy-start.41
  47.5 4.1 copy-start.55
  51.6 7.9 %copy-start.62 = (f32[1,4096]{1,0:T(1,128)S(1)}, f32[1,4096]{1,0:T(1,128)}, u32[]{:S(2)}) copy-start(f32[1,4096]{1,0:T(1,128)} %get-tuple-element.53) | copy-start | bytes 49156
  58.8 10.6 %copy-start.28 = (bf16[1,256,2560]{2,1,0:T(8,128)(2,1)}, bf16[1,256,2560]{2,1,0:T(8,128)(2,1)S(1)}, u32[]{:S(2)}) copy-start(bf16[1,256,2560]{2,1,0:T(8,128)(2,1)S(1)} %get-tuple-element.64) | copy-start | bytes 3932164
  59.4 10.0 %copy-start.69 = (f32[256]{0:T(256)}, f32[256]{0:T(256)S(1)}, u32[]{:S(2)}) copy-start(f32[256]{0:T(256)S(1)} %get-tuple-element.60) | copy-start | bytes 3076
  74.0 490.5 %reduce-scatter.2.cloned.1.call-start = ((), (), s32[]{:S(2)}) async-start(), calls=%async_computation.2 | async-start | bytes 34603008 | tf_op jit(solution)/shard_map/reduce_scatter | solution.py:137
  74.4 161.6 %copy-start.59 = (f32[4,2]{1,0:T(4,128)}, f32[4,2]{1,0:T(4,128)S(1)}, u32[]{:S(2)}) copy-start(f32[4,2]{1,0:T(4,128)S(1)} %max.58) | copy-start | bytes 100
  214.3 21.7 %copy-start.49 = (f32[4,2,256]{2,1,0:T(2,128)}, f32[4,2,256]{2,1,0:T(2,128)S(1)}, u32[]{:S(2)}) copy-start(f32[4,2,256]{2,1,0:T(2,128)S(1)} %get-tuple-element.65) | copy-start | bytes 24580
  214.4 21.8 %copy-start.33 = (bf16[256,2048]{0,1:T(8,128)(2,1)S(1)}, bf16[256,2048]{0,1:T(8,128)(2,1)}, u32[]{:S(2)}) copy-start(bf16[256,2048]{0,1:T(8,128)(2,1)} %copy.141) | copy-start | bytes 3145732
  236.0 32.2 %copy-start.45 = (f32[4,2,256]{2,1,0:T(2,128)}, f32[4,2,256]{2,1,0:T(2,128)S(1)}, u32[]{:S(2)}) copy-start(f32[4,2,256]{2,1,0:T(2,128)S(1)} %fusion.6) | copy-start | bytes 24580
  312.5 43.7 %copy-start.37 = (bf16[256,4,2,128]{3,0,2,1:T(8,128)(2,1)S(1)}, bf16[256,4,2,128]{3,0,2,1:T(8,128)(2,1)}, u32[]{:S(2)}) copy-start(bf16[256,4,2,128]{3,0,2,1:T(8,128)(2,1)} %get-tuple-element.22) | copy-start | bytes 1572868
  312.5 43.7 %copy-start.38 = (bf16[256,4,2,128]{3,0,2,1:T(8,128)(2,1)S(1)}, bf16[256,4,2,128]{3,0,2,1:T(8,128)(2,1)}, u32[]{:S(2)}) copy-start(bf16[256,4,2,128]{3,0,2,1:T(8,128)(2,1)} %get-tuple-element.23) | copy-start | bytes 1572868
  409.5 20.6 %copy-start.4 = (f32[256,128]{1,0:T(8,128)S(1)}, f32[256,128]{1,0:T(8,128)}, u32[]{:S(2)}) copy-start(f32[256,128]{1,0:T(8,128)} %copy-done.3) | copy-start | bytes 393220
  409.5 20.6 %copy-start.19 = (f32[256,128]{1,0:T(8,128)S(1)}, f32[256,128]{1,0:T(8,128)}, u32[]{:S(2)}) copy-start(f32[256,128]{1,0:T(8,128)} %get-tuple-element.54) | copy-start | bytes 393220
  431.8 4.4 copy-start.46
  431.8 4.4 copy-start.50
  431.9 4.4 copy-start.60
  442.6 30.7 %copy-start.63 = (f32[2560]{0:T(1024)S(1)}, f32[2560]{0:T(1024)}, u32[]{:S(2)}) copy-start(f32[2560]{0:T(1024)} %get-tuple-element.10) | copy-start | bytes 30724
  569.4 11.6 %copy-start.68 = (f32[256]{0:T(256)S(1)}, f32[256]{0:T(256)}, u32[]{:S(2)}) copy-start(f32[256]{0:T(256)} %get-tuple-element.59) | copy-start | bytes 3076
  585.2 10.6 %copy-start.1 = (f32[4,384,256,2]{2,1,3,0:T(8,128)S(1)}, f32[4,384,256,2]{2,1,3,0:T(8,128)}, u32[]{:S(2)}) copy-start(f32[4,384,256,2]{2,1,3,0:T(8,128)} %copy-done) | copy-start | bytes 9437188
  585.2 10.6 %copy-start.36 = (pred[256,384]{0,1:T(8,128)(4,1)S(1)}, pred[256,384]{0,1:T(8,128)(4,1)}, u32[]{:S(2)}) copy-start(pred[256,384]{0,1:T(8,128)(4,1)} %copy-done.35) | copy-start | bytes 294916
  585.2 10.6 %copy-start.42 = (f32[4,2,256]{2,1,0:T(2,128)S(1)}, f32[4,2,256]{2,1,0:T(2,128)}, u32[]{:S(2)}) copy-start(f32[4,2,256]{2,1,0:T(2,128)} %copy-done.41) | copy-start | bytes 24580
  585.2 10.6 %copy-start.56 = (f32[4,2,256]{2,1,0:T(2,128)S(1)}, f32[4,2,256]{2,1,0:T(2,128)}, u32[]{:S(2)}) copy-start(f32[4,2,256]{2,1,0:T(2,128)} %copy-done.55) | copy-start | bytes 24580
  595.8 2.7 copy-start.44
  595.8 2.7 copy-start.48
  609.4 6.2 copy-start.71
  612.1 17.1 %collective-permute-start.1 = (bf16[1,128,8,256]{3,1,2,0:T(8,128)(2,1)}, bf16[1,128,8,256]{3,1,2,0:T(8,128)(2,1)}, u32[]{:S(2)}, u32[]{:S(2)}) collective-permute-start(bf16[1,128,8,256]{3,1,2,0:T(8,128)(2,1)} %get-tuple-element.31), channel_id=1, source_target_pairs={{1,0},{2,1},{3,2},{4,3},{5,4},{6,5},{7,6},{8,7},{9,8},{10,9},{11,1... | collective-permute-start | bytes 1572872 | tf_op jit(solution)/shard_map/ppermute | solution.py:145
  616.2 5.8 copy-start.17
  619.4 6.2 copy-start.64
  623.3 5.9 copy-start.8
  631.7 4.7 copy-start.10
  631.8 4.7 copy-start.52
  631.8 4.7 copy-start.67
  636.5 12.1 %copy-start.6 = (f32[1,256,4,2,256]{1,4,3,2,0:T(8,128)S(1)}, f32[1,256,4,2,256]{1,4,3,2,0:T(8,128)}, u32[]{:S(2)}) copy-start(f32[1,256,4,2,256]{1,4,3,2,0:T(8,128)} %copy.90) | copy-start | bytes 6291460
  648.6 3.6 copy-start.12
  648.6 3.6 copy-start.21
  648.6 3.6 copy-start.65
  (31 other events, 53.2 us)
Sparse Core Ops, SparseCore 0:
  74.1 110.9 all-gather.1
  409.6 154.9 reduce-scatter.1
where the time goes:
time: 667 us; the launch traced here: 662 us
  matrix products  272 us (41%)
  waiting for transfers between devices  168 us (25%)
  other arithmetic  130 us (19%)
  local copies, waits for them, and re-layouts  67.1 us (10%)
  between operations  15.6 us (2%)
  starting transfers between devices  8.58 us (1%)
    all_gather x1, waiting for transfers between devices, local_step(): lax.all_gather(jnp.concatenate([keys_two, values_two], axis=2), 'cp', axi...  85.3 us
    reduce_scatter x1, waiting for transfers between devices, local_step(): lax.psum_scatter(jnp.concatenate([dk_far, dv_far], axis=2).astype(jnp.bfl...  82.9 us
    another operation x10, other arithmetic  50.2 us
    dot_general x2, matrix products, attend_backward(): jnp.einsum('bqkgd,bskd->bkgqs', d_attn, value_rows, preferred_element_typ...  47 us
    dot_general x2, matrix products, attend_backward(): jnp.einsum('bkgqs,bqkgd->bskd', prob_bf, d_attn, preferred_element_type=j...  34.2 us
    dot_general x2, matrix products, attend_forward(): jnp.einsum('bkgqs,bskd->bqkgd', prob_bf, value_rows, preferred_element_ty...  33 us
    dot_general x2, matrix products, attend_forward(): jnp.einsum('bqkgd,bskd->bkgqs', query_rows, key_rows, preferred_element_t...  31 us
    dot_general x2, matrix products, attend_backward(): jnp.einsum('bkgqs,bqkgd->bskd', d_scores, query_rows, preferred_element_t...  30.9 us
  transfers between devices with their start and end apart: 4, of which 2 were waited for; matrix products, arithmetic and copies ran while one was open for 18% of the time, Pallas kernels for 0%

commit v1 on v0

--- a/solution.py
+++ b/solution.py
@@ -1,7 +1,11 @@
+import functools
+
 import jax
 import jax.numpy as jnp
 import math
 from jax import lax
+from jax.experimental import pallas as pl
+from jax.experimental.pallas import tpu as pltpu
 from jax.sharding import PartitionSpec as P
 
 WINDOW = 128
@@ -94,6 +98,317 @@
     return jnp.dot(attn_out.reshape(batch_size, seq_dev, -1), w_proj, preferred_element_type=jnp.float32) + bias_row
 
 
+MESH = pl.DeviceIdType.MESH
+F32 = jnp.float32
+BF16 = jnp.bfloat16
+
+
+def far_attention_kernel(dims, sink_ref, q_ref, kv_ref, do_ref, o_out, dq_out, dkv_out, dsink_out,
+                         q_all, do_all, kv_all, o_acc, dq_acc, m_ref, l_ref, delta_ref,
+                         d_acc, o_stage, ds_stage, sib_send, sib_recv, far_send, far_recv, near_send, near_recv,
+                         y_ssem, y_rsem, sib_ssem, sib_rsem, near_ssem, near_rsem, relay_ssem, relay_rsem,
+                         bsib_ssem, bsib_rsem, bfar_ssem, bfar_rsem, bnear_ssem, bnear_rsem):
+    heads, cores, cols, rows, width = dims
+    pair = cores * rows
+    scale = width ** -0.5
+    me = lax.axis_index('cp')
+    core = lax.rem(me, cores)
+    x = lax.rem(me // cores, cols)
+    y = me // (cores * cols)
+    sib = lax.rem(core + 1, cores)
+
+    def device(yy, xx, cc):
+        return (yy * cols + xx) * cores + cc
+
+    right = lax.rem(x + 1, cols)
+    left = lax.rem(x + cols - 1, cols)
+    far = lax.rem(x + 2, cols)
+    offsets = [(dy, dc) for dy in (1, 3, 2, 0) for dc in range(cores) if (dy, dc) != (0, 0)]
+
+    barrier = pltpu.get_barrier_semaphore()
+    partners = [device(lax.rem(y + dy, heads), x, lax.rem(core + dc, cores)) for dy, dc in offsets]
+    partners += [device(y, right, core), device(y, left, core)]
+    for other in partners:
+        pl.semaphore_signal(barrier, inc=1, device_id={'cp': other}, device_id_type=MESH)
+    pl.semaphore_wait(barrier, len(partners))
+
+    def remote(src, dst, ssem, rsem, target):
+        return pltpu.make_async_remote_copy(src_ref=src, dst_ref=dst, send_sem=ssem, recv_sem=rsem,
+                                            device_id={'cp': target}, device_id_type=MESH)
+
+    pending = []
+
+    def exchange(kind, src_of, dst_of):
+        copies = {}
+        for dy, dc in offsets + [(0, 0)]:
+            ty, tc = lax.rem(y + dy, heads), lax.rem(core + dc, cores)
+            if (dy, dc) == (0, 0):
+                copy = pltpu.make_async_copy(src_of(ty, tc), dst_of(ty, tc), y_rsem.at[kind, dy, dc])
+            else:
+                copy = remote(src_of(ty, tc), dst_of(ty, tc), y_ssem.at[kind, dy, dc], y_rsem.at[kind, dy, dc], device(ty, x, tc))
+                pending.append(copy)
+            copy.start()
+            copies[dy, dc] = copy
+        return copies
+
+    def arrive(copies, key):
+        if key == (0, 0):
+            copies[key].wait()
+        else:
+            copies[key].wait_recv()
+
+    def lanes(block, size):
+        return pl.ds(pl.multiple_of(block * size, size), size)
+
+    my_rows = lanes(core, rows)
+    kv_copies = exchange(0, lambda ty, tc: kv_ref.at[:, lanes(tc * heads + ty, width)],
+                         lambda ty, tc: kv_all.at[tc, x, y, my_rows])
+    q_copies = exchange(1, lambda ty, tc: q_ref.at[:, lanes(ty * cores + tc, width)],
+                        lambda ty, tc: q_all.at[y, my_rows])
+    do_copies = exchange(2, lambda ty, tc: do_ref.at[:, lanes(ty * cores + tc, width)],
+                         lambda ty, tc: do_all.at[y, my_rows])
+
+    sink = sink_ref[y * cores + core]
+    m_ref[...] = jnp.zeros_like(m_ref) + sink
+    l_ref[...] = jnp.ones_like(l_ref)
+    o_acc[...] = jnp.zeros_like(o_acc)
+    dq_acc[...] = jnp.zeros_like(dq_acc)
+
+    order = (0, 1, 3, 2)
+    sib_copies = {}
+    near_copies = {}
+    relay_copies = {}
+
+    def to_sibling(rel, col, dy, piece):
+        copy = remote(kv_all.at[core, col, piece], kv_all.at[core, col, piece], sib_ssem.at[rel, dy], sib_rsem.at[rel, dy], device(y, x, sib))
+        copy.start()
+        pending.append(copy)
+        sib_copies[rel, dy] = copy
+
+    def piece_of(dy):
+        return lax.rem(y + heads - dy, heads)
+
+    for dy in order:
+        for dc in range(cores):
+            arrive(kv_copies, (dy, dc))
+        piece = piece_of(dy)
+        for way, col in ((0, right), (1, left)):
+            copy = remote(kv_all.at[core, x, piece], kv_all.at[core, x, piece], near_ssem.at[way, dy], near_rsem.at[way, dy], device(y, col, core))
+            copy.start()
+            pending.append(copy)
+            near_copies[way, dy] = copy
+        to_sibling(0, x, dy, piece)
+
+    def relay(dy):
+        piece = piece_of(dy)
+        near_copies[0, dy].wait_recv()
+        if dy in (0, 1):
+            copy = remote(kv_all.at[core, left, piece], kv_all.at[core, left, piece], relay_ssem.at[dy], relay_rsem.at[dy], device(y, right, core))
+            copy.start()
+            pending.append(copy)
+            relay_copies[dy] = copy
+        to_sibling(3, left, dy, piece)
+        near_copies[1, dy].wait_recv()
+        if dy in (2, 3):
+            copy = remote(kv_all.at[core, right, piece], kv_all.at[core, right, piece], relay_ssem.at[dy], relay_rsem.at[dy], device(y, left, core))
+            copy.start()
+            pending.append(copy)
+            relay_copies[dy] = copy
+        to_sibling(1, right, dy, piece)
+
+    def scores(key_blk, query_blk, masked):
+        out = lax.dot_general(key_blk, query_blk, (((1,), (1,)), ((), ())), preferred_element_type=F32) * scale
+        if masked:
+            key_pos = lax.broadcasted_iota(jnp.int32, out.shape, 0)
+            query_pos = lax.broadcasted_iota(jnp.int32, out.shape, 1)
+            out = jnp.where(key_pos <= query_pos, out, -jnp.inf)
+        return out
+
+    def forward_block(col, yk, yq, masked):
+        value_blk = kv_all[1, col, yk]
+        logits = scores(kv_all[0, col, yk], q_all[yq], masked)
+        old_peak = m_ref[yq]
+        peak = jnp.maximum(old_peak, jnp.max(logits, axis=0, keepdims=True))
+        shrink = jnp.exp(old_peak - peak)
+        weight = jnp.exp(logits - peak)
+        m_ref[yq] = peak
+        l_ref[yq] = l_ref[yq] * shrink + jnp.sum(weight, axis=0, keepdims=True)
+        o_acc[yq] = o_acc[yq] * shrink + lax.dot_general(value_blk, weight.astype(BF16), (((0,), (0,)), ((), ())), preferred_element_type=F32)
+
+    def backward_block(rel, col, yk, yq, masked):
+        key_blk, value_blk = kv_all[0, col, yk], kv_all[1, col, yk]
+        query_blk, grad_blk = q_all[yq], do_all[yq]
+        prob = jnp.exp(scores(key_blk, query_blk, masked) - m_ref[yq])
+        d_prob = lax.dot_general(value_blk, grad_blk, (((1,), (1,)), ((), ())), preferred_element_type=F32).astype(BF16).astype(F32)
+        d_score = (prob * (d_prob - delta_ref[yq])).astype(BF16)
+        d_acc[rel, 1, yk] += jnp.dot(prob.astype(BF16), grad_blk, preferred_element_type=F32)
+        d_acc[rel, 0, yk] += jnp.dot(d_score, query_blk, preferred_element_type=F32)
+        dq_acc[yq] += lax.dot_general(key_blk, d_score, (((0,), (0,)), ((), ())), preferred_element_type=F32)
+
+    def sweep(block, rel, col):
+        skip = 1 if rel == 0 else jnp.where(col > x, 1, 0)
+
+        def over_keys(yk, carry):
+            if rel == 0:
+                block(yk, yk, True)
+
+            def over_queries(yq, inner):
+                block(yk, yq, False)
+                return inner
+
+            lax.fori_loop(yk + skip, heads, over_queries, 0)
+            return carry
+
+        lax.fori_loop(0, heads, over_keys, 0)
+
+    cols_of = {0: x, 1: right, 2: far, 3: left}
+
+    def forward(rel):
+        col = cols_of[rel]
+        sweep(lambda yk, yq, masked: forward_block(col, yk, yq, masked), rel, col)
+
+    def backward(rel):
+        col = cols_of[rel]
+        sweep(lambda yk, yq, masked: backward_block(rel, col, yk, yq, masked), rel, col)
+
+    def await_sibling(rel):
+        for dy in order:
+            sib_copies[rel, dy].wait_recv()
+
+    relay(0)
+    relay(1)
+    for key in offsets + [(0, 0)]:
+        arrive(q_copies, key)
+    await_sibling(0)
+    forward(0)
+    relay(3)
+    relay(2)
+    d_acc[...] = jnp.zeros_like(d_acc)
+    await_sibling(1)
+    await_sibling(3)
+    forward(1)
+    forward(3)
+    for dy in order:
+        relay_copies[dy].wait_recv()
+        to_sibling(2, far, dy, piece_of(dy))
+    await_sibling(2)
+    forward(2)
+
+    for key in offsets + [(0, 0)]:
+        arrive(do_copies, key)
+
+    def finish_forward(yq, carry):
+        attn = o_acc[yq] / l_ref[yq]
+        lse = m_ref[yq] + jnp.log(l_ref[yq])
+        delta = jnp.sum(attn * jnp.transpose(do_all[yq].astype(F32)), axis=0, keepdims=True)
+        o_stage[0, yq] = jnp.transpose(attn).astype(BF16)
+        m_ref[yq] = lse
+        delta_ref[yq] = delta
+        contribution = -jnp.exp(sink - lse) * delta
+        for part in range(cores):
+            total = jnp.sum(contribution[:, part * rows:(part + 1) * rows], axis=1, keepdims=True)
+            ds_stage[yq * cores + part] = jnp.zeros(ds_stage.shape[1:], F32) + total
+        return carry
+
+    lax.fori_loop(0, heads, finish_forward, 0)
+
+    mine = y * cores + core
+    o_copies = exchange(3, lambda ty, tc: o_stage.at[0, ty, lanes(tc, rows)], lambda ty, tc: o_out.at[:, lanes(mine, width)])
+    ds_copies = exchange(4, lambda ty, tc: ds_stage.at[ty * cores + tc], lambda ty, tc: dsink_out.at[mine])
+
+    bsib_copies = {}
+
+    def swap_partial(rel):
+        sib_send[rel] = d_acc[rel, sib].astype(BF16)
+        copy = remote(sib_send.at[rel], sib_recv.at[rel], bsib_ssem.at[rel], bsib_rsem.at[rel], device(y, x, sib))
+        copy.start()
+        pending.append(copy)
+        bsib_copies[rel] = copy
+
+    half = heads // 2
+    backward(2)
+    swap_partial(2)
+    backward(3)
+    swap_partial(3)
+    bsib_copies[2].wait_recv()
+    far_send[...] = (d_acc[2, core] + sib_recv[2].astype(F32)).astype(BF16)
+    bfar = {}
+    for way, col, start in ((0, right, 0), (1, left, half)):
+        copy = remote(far_send.at[pl.ds(start, half)], far_recv.at[way], bfar_ssem.at[way], bfar_rsem.at[way], device(y, col, core))
+        copy.start()
+        pending.append(copy)
+        bfar[way] = copy
+    backward(1)
+    swap_partial(1)
+    bnear = {}
+    for way, rel, col, start in ((1, 3, left, half), (0, 1, right, 0)):
+        bsib_copies[rel].wait_recv()
+        bfar[way].wait_recv()
+        total = d_acc[rel, core] + sib_recv[rel].astype(F32)
+        near_send[way] = total.astype(BF16)
+        near_send[way, start:start + half] = (total[start:start + half] + far_recv[way].astype(F32)).astype(BF16)
+        copy = remote(near_send.at[way], near_recv.at[way], bnear_ssem.at[way], bnear_rsem.at[way], device(y, col, core))
+        copy.start()
+        pending.append(copy)
+        bnear[way] = copy
+    backward(0)
+    swap_partial(0)
+
+    def finish_backward(yq, carry):
+        o_stage[1, yq] = jnp.transpose(dq_acc[yq] * scale).astype(BF16)
+        return carry
+
+    lax.fori_loop(0, heads, finish_backward, 0)
+    dq_copies = exchange(5, lambda ty, tc: o_stage.at[1, ty, lanes(tc, rows)], lambda ty, tc: dq_out.at[:, lanes(mine, width)])
+
+    bsib_copies[0].wait_recv()
+    bnear[0].wait_recv()
+    bnear[1].wait_recv()
+    factor = jnp.where(core == 0, scale, 1.0)
+    o_stage[2] = ((d_acc[0, core] + sib_recv[0].astype(F32) + near_recv[0].astype(F32) + near_recv[1].astype(F32)) * factor).astype(BF16)
+    dkv_copies = exchange(6, lambda ty, tc: o_stage.at[2, ty, lanes(tc, rows)], lambda ty, tc: dkv_out.at[:, lanes(core * heads + y, width)])
+
+    for copies in (o_copies, ds_copies, dq_copies, dkv_copies):
+        for key in offsets + [(0, 0)]:
+            arrive(copies, key)
+    for copy in pending:
+        copy.wait_send()
+
+
+def far_attention(q2, kv2, do2, sinks, kv_heads, num_shards):
+    rows = q2.shape[0]
+    num_heads = sinks.shape[0]
+    width = q2.shape[1] // num_heads
+    cores = num_heads // kv_heads
+    cols = num_shards // num_heads
+    assert cols == 4 and kv_heads == 4 and cores == 2
+    pair = cores * rows
+    full = (kv_heads, pair, width)
+    vm, dma = pltpu.VMEM, pltpu.SemaphoreType.DMA
+    scratch = [
+        vm(full, BF16), vm(full, BF16), vm((2, cols) + full, BF16),
+        vm((kv_heads, width, pair), F32), vm((kv_heads, width, pair), F32),
+        vm((kv_heads, 1, pair), F32), vm((kv_heads, 1, pair), F32), vm((kv_heads, 1, pair), F32),
+        vm((cols, 2) + full, F32), vm((3,) + full, BF16), vm((num_heads, 8, 128), F32),
+        vm((cols,) + full, BF16), vm((cols,) + full, BF16), vm(full, BF16), vm((2, kv_heads // 2, pair, width), BF16),
+        vm((2,) + full, BF16), vm((2,) + full, BF16),
+        dma((7, kv_heads, cores)), dma((7, kv_heads, cores)), dma((cols, kv_heads)), dma((cols, kv_heads)),
+        dma((2, kv_heads)), dma((2, kv_heads)), dma((kv_heads,)), dma((kv_heads,)),
+        dma((cols,)), dma((cols,)), dma((2,)), dma((2,)), dma((2,)), dma((2,)),
+    ]
+    space = pl.BlockSpec(memory_space=pltpu.VMEM)
+    return pl.pallas_call(
+        functools.partial(far_attention_kernel, (kv_heads, cores, cols, rows, width)),
+        out_shape=[jax.ShapeDtypeStruct((rows, num_heads * width), BF16), jax.ShapeDtypeStruct((rows, num_heads * width), BF16),
+                   jax.ShapeDtypeStruct((rows, 2 * kv_heads * width), BF16), jax.ShapeDtypeStruct((num_heads, 8, 128), F32)],
+        in_specs=[pl.BlockSpec(memory_space=pltpu.SMEM), space, space, space],
+        out_specs=[space] * 4,
+        scratch_shapes=scratch,
+        compiler_params=pltpu.CompilerParams(collective_id=0, has_side_effects=True, vmem_limit_bytes=67043328),
+        name='far_attention',
+    )(sinks, q2, kv2, do2)
+
+
 def solution(mesh):
     num_shards = mesh.shape['cp']
     forward_pairs = [(source, source + 1) for source in range(num_shards - 1)]
@@ -124,17 +439,15 @@
 
         hid_two = middle.astype(jnp.float32)
         query_two, keys_two, values_two, rms_two = norm_project(hid_two, norm_gain[1], w_qkv[1], b_qkv[1], cos_tab, sin_tab, num_heads, kv_heads)
-        all_rows = lax.all_gather(jnp.concatenate([keys_two, values_two], axis=2), 'cp', axis=1, tiled=True)
-        far_keys = all_rows[:, :, :kv_heads]
-        far_values = all_rows[:, :, kv_heads:]
-        far_pos = jnp.arange(all_rows.shape[1])
-        attn_two, prob_two, probbf_two, sink_two = attend_forward(query_two, far_keys, far_values, attn_sinks[1], row_pos, far_pos, False, logit_scale)
+        d_out_two = grad_out.astype(jnp.float32)
+        d_attn_two = jnp.einsum('bsd,qd->bsq', grad_out, w_out[1], preferred_element_type=jnp.float32).astype(jnp.bfloat16)
+        flat_two = jnp.concatenate([keys_two.reshape(seq_dev, -1), values_two.reshape(seq_dev, -1)], axis=1)
+        attn_two, dq_two, own_two, dsink_wide = far_attention(query_two.reshape(seq_dev, -1), flat_two, d_attn_two.reshape(seq_dev, -1), attn_sinks[1], kv_heads, num_shards)
+        attn_two = attn_two.reshape(1, seq_dev, -1)
+        dq_two = dq_two.reshape(query_two.shape)
+        own_two = own_two.reshape(1, seq_dev, 2 * kv_heads, head_dim)
+        dsink_two = dsink_wide[:, 0, 0]
         output = (hid_two + dense_out(attn_two, w_out[1], b_out[1])).astype(jnp.bfloat16)
-
-        d_out_two = grad_out.astype(jnp.float32)
-        d_attn_two = jnp.einsum('bsd,qd->bsq', grad_out, w_out[1], preferred_element_type=jnp.float32).astype(jnp.bfloat16).reshape(query_two.shape)
-        dq_two, dk_far, dv_far, dsink_two = attend_backward(d_attn_two, query_two, far_keys, far_values, prob_two, probbf_two, sink_two, logit_scale)
-        own_two = lax.psum_scatter(jnp.concatenate([dk_far, dv_far], axis=2).astype(jnp.bfloat16), 'cp', scatter_dimension=1, tiled=True)
         dhid_two, dgain_two, dbias_two = project_backward(dq_two, own_two[:, :, :kv_heads], own_two[:, :, kv_heads:], hid_two, rms_two, norm_gain[1], w_qkv[1], cos_tab, sin_tab)
         d_middle = (d_out_two + dhid_two).astype(jnp.bfloat16)
 

time: 667 us -> 336 us (0.50)
  the two profiles are of different devices: /device:TPU:97 before, /device:TPU:104 now
where the time goes in v1:
time: 336 us; the launch traced here: 331 us
  Pallas kernels  141 us (42%)
  matrix products  83.1 us (25%)
  local copies, waits for them, and re-layouts  61.2 us (18%)
  other arithmetic  32.2 us (10%)
  starting transfers between devices  11 us (3%)
    pallas_call x1, Pallas kernels, far_attention(): pl.pallas_call(functools.partial(far_attention_kernel, (kv_heads, cores,...  141 us
    dot_general x2, matrix products, project_backward(): jnp.einsum('bsq,dq->bsd', d_proj.astype(jnp.bfloat16), w_in, preferred_el...  23.9 us
    dot_general x2, matrix products, norm_project(): jnp.dot(normed, w_in, preferred_element_type=jnp.float32) + bias_row  20.2 us
    dot_general x2, matrix products, dense_out(): jnp.dot(attn_out.reshape(batch_size, seq_dev, -1), w_proj, preferred_elem...  15.2 us
    concatenate x6, local copies, waits for them, and re-layouts, rotate_half(): jnp.concatenate([first_half * cos_tab - second_half * sin_tab, second_hal...  11.4 us
    another operation x5, local copies, waits for them, and re-layouts  9.11 us
    ppermute x1, starting transfers between devices, local_step(): lax.ppermute(near_grad[:, :WINDOW].astype(jnp.bfloat16), 'cp', backward_p...  9.03 us
    dot_general x1, matrix products, local_step(): jnp.einsum('bsd,qd->bsq', d_middle, w_out[0], preferred_element_type=jnp....  8 us
  transfers between devices with their start and end apart: 2, of which 0 were waited for; matrix products, arithmetic and copies ran while one was open for 12% of the time, Pallas kernels for 0%

profile of v1, /device:TPU:104, one launch (start us, length us, event | category | flops | bytes accessed | tf_op | source)
XLA Modules:
  0.0 330.6 jit_solution(12306836438741056642)
XLA Ops:
  0.7 1.7 fusion.80
  4.6 10.3 %fusion.27 = f32[1,256,4096]{2,1,0:T(8,128)S(1)} fusion(bf16[2,2560,4096]{2,1,0:T(8,128)(2,1)} %param.11, f32[4096]{0:T(1024)S(1)} %bitcast.272, bf16[1,256,2560]{2,1,0:T(8,128)(2,1)} %param.8, f32[2560]{0:T(1024)S(1)} %get-tuple-element.21, f32[256]{0:T(256)S(1)} %get-tuple-element.65), kind=kOutput, calls=%fused_computation.37 | convolution fusion | flops 5372379136 | bytes 26504192 | tf_op jit(solution)/shard_map/dot_general | solution.py:47
  15.0 1.9 copy-done.5
  19.0 1.2 fusion.149
  21.3 1.9 collective-permute-start
  25.2 3.0 reshape.674
  28.1 2.4 fusion.178
  30.5 7.9 %fusion.99.do_ref = bf16[256,2048]{1,0:T(8,128)(2,1)} fusion(bf16[2,2048,2560]{2,1,0:T(8,128)(2,1)} %param.13, bf16[1,256,2560]{2,1,0:T(8,128)(2,1)S(1)} %copy-done.19), kind=kOutput, calls=%fused_computation.89 | convolution fusion | flops 2684878848 | bytes 12845056 | tf_op jit(solution)/shard_map/bsd,qd->bsq/dot_general | solution.py:443
  39.0 1.4 fusion.183
  42.3 1.1 fusion.119
  43.8 7.2 %fusion.88 = (f32[256]{0:T(256)S(1)}, bf16[1,256,2560]{2,1,0:T(8,128)(2,1)S(1)}) fusion(f32[2560]{0:T(1024)S(1)} %get-tuple-element.19, bf16[256,2048]{0,1:T(8,128)(2,1)S(1)} %bitcast.274, bf16[2,2048,2560]{2,1,0:T(8,128)(2,1)} %param.13, bf16[1,256,2560]{2,1,0:T(8,128)(2,1)S(1)} %copy-done.7), kind=kOutput, calls=%fused_computation.80 | convolution fusion | flops 2688941824 | bytes 14167040 | tf_op jit(solution)/shard_map/dot_general | solution.py:98
  51.6 9.9 %fusion.33 = f32[1,256,4096]{2,1,0:T(8,128)S(1)} fusion(bf16[2,2560,4096]{2,1,0:T(8,128)(2,1)} %param.11, f32[4096]{0:T(1024)S(1)} %bitcast.271, bf16[1,256,2560]{2,1,0:T(8,128)(2,1)S(1)} %get-tuple-element.73, f32[2560]{0:T(1024)S(1)} %get-tuple-element.20, f32[256]{0:T(256)S(1)} %get-tuple-element.67), kind=kOutput, calls=%fused_computation.39 | convolution fusion | flops 5372379136 | bytes 26504192 | tf_op jit(solution)/shard_map/dot_general | solution.py:47
  62.5 1.5 slice.207
  64.0 3.4 %reshape.678 = f32[1,256,4,2,256]{4,3,2,1,0:T(2,128)S(1)} reshape(f32[1,256,2048]{2,1,0:T(8,128)} %slice.207) | data formatting | bytes 4194304 | tf_op jit(solution)/shard_map/reshape | solution.py:48
  67.4 1.4 reshape.679
  68.9 1.3 fusion.181
  72.2 1.1 copy.131
  73.3 1.6 convert_element_type.209.q_ref
  74.9 1.1 pad_maximum_fusion.5.kv_ref
  76.0 140.8 %far_attention.1 = (bf16[256,2048]{1,0:T(8,128)(2,1)}, bf16[256,2048]{1,0:T(8,128)(2,1)}, bf16[256,2048]{1,0:T(8,128)(2,1)}, f32[8,8,128]{2,1,0:T(8,128)}) custom-call(f32[8]{0:T(128)} %get-tuple-element.69.sink_ref, bf16[256,2048]{1,0:T(8,128)(2,1)} %convert_element_type.209.q_ref, bf16[256,2048]{1,0:T(8,128)(2,1)} %pad_maximum_fusion.5.kv_ref, ...), custom_call_target="tpu_custom_call" | custom-call | tf_op jit(solution)/shard_map/far_attention/pallas_call | solution.py:400
  216.8 1.6 copy.196
  221.5 3.1 reshape.693
  225.9 1.5 pad_maximum_fusion.1
  228.3 1.3 copy.137
  229.7 11.8 %fusion.95 = (f32[2560]{0:T(1024)}, f32[256]{0:T(256)S(1)}, f32[256,2560]{1,0:T(8,128)S(1)}) fusion(bf16[1,256,2560]{2,1,0:T(8,128)(2,1)} %copy-done.20, f32[256]{0:T(256)S(1)} %copy-done.58, f32[2560]{0:T(1024)S(1)} %copy-done.45, bf16[2,2560,4096]{2,1,0:T(8,128)(2,1)} %param.11, bf16[256,1024]{0,1:T(8,128)(2,1)S(1)} %bitcast.265, ...), kind=kOutput, calls=%fused_computation.87 | convolution fusion | flops 5380895744 | bytes 27023360 | tf_op jit(solution)/shard_map/bsq,dq->bsd/dot_general | solution.py:89
  241.4 3.2 convert_reduce_fusion
  244.6 1.1 copy-done.9
  245.8 8.0 %fusion.96 = bf16[256,2048]{1,0:T(8,128)(2,1)} fusion(bf16[2,2048,2560]{2,1,0:T(8,128)(2,1)} %param.13, bf16[1,256,2560]{2,1,0:T(8,128)(2,1)S(1)} %get-tuple-element.23), kind=kOutput, calls=%fused_computation.88 | convolution fusion | flops 2684878848 | bytes 12845056 | tf_op jit(solution)/shard_map/bsd,qd->bsq/dot_general | solution.py:455
  253.8 2.5 copy.194
  256.3 2.8 fusion.73
  259.1 2.1 fusion.122
  264.8 1.2 fusion.173
  266.0 1.5 pad_maximum_fusion.2
  269.8 9.0 %collective-permute-start.1 = (bf16[1,128,8,256]{3,1,2,0:T(8,128)(2,1)}, bf16[1,128,8,256]{3,1,2,0:T(8,128)(2,1)}, u32[]{:S(2)}, u32[]{:S(2)}) collective-permute-start(bf16[1,128,8,256]{3,1,2,0:T(8,128)(2,1)} %get-tuple-element.39), channel_id=1, source_target_pairs={{1,0},{2,1},{3,2},{4,3},{5,4},{6,5},{7,6},{8,7},{9,8},{10,9},{11,1... | collective-permute-start | bytes 1572872 | tf_op jit(solution)/shard_map/ppermute | solution.py:458
  278.8 8.0 %fusion.55 = bf16[1,256,2560]{2,1,0:T(8,128)(2,1)} fusion(bf16[256,2048]{1,0:T(8,128)(2,1)S(1)} %copy-done.60, bf16[2,2048,2560]{2,1,0:T(8,128)(2,1)} %param.13, bf16[1,256,2560]{2,1,0:T(8,128)(2,1)S(1)} %copy-done.21, f32[2560]{0:T(1024)S(1)} %copy-done.51), kind=kOutput, calls=%fused_computation.47 | convolution fusion | flops 2686976000 | bytes 14166016 | tf_op jit(solution)/shard_map/dot_general | solution.py:98
  287.4 2.5 copy.160
  289.9 2.5 copy.161
  292.4 3.1 copy.159
  295.6 2.9 copy.156
  298.5 2.3 copy.147
  300.8 2.8 maximum_reduce_fusion.1
  304.3 1.2 fusion.139
  307.6 1.2 copy.158
  308.8 1.3 copy.157
  310.2 2.1 copy.154
  312.2 12.1 %fusion.87 = (f32[2560]{0:T(1024)S(1)}, f32[256]{0:T(256)S(1)}, f32[256,2560]{1,0:T(8,128)}) fusion(bf16[1,256,2560]{2,1,0:T(8,128)(2,1)S(1)} %copy-done.8, f32[256]{0:T(256)S(1)} %copy-done.55, f32[2560]{0:T(1024)S(1)} %copy-done.43, bf16[2,2560,4096]{2,1,0:T(8,128)(2,1)} %param.11, bf16[256,1024]{0,1:T(8,128)(2,1)} %bitcast.266, ...), kind=kOutput, calls=%fused_computation.79 | convolution fusion | flops 5380895744 | bytes 27023360 | tf_op jit(solution)/shard_map/bsq,dq->bsd/dot_general | solution.py:89
  324.4 2.3 maximum_reduce_fusion
  328.0 2.1 fusion.79
  (199 shorter events, 29.2 us)
Async XLA Ops:
  2.9 12.1 %copy-start.54 = (f32[256]{0:T(256)}, f32[256]{0:T(256)S(1)}, u32[]{:S(2)}) copy-start(f32[256]{0:T(256)S(1)} %get-tuple-element.65) | copy-start | bytes 3076
  3.7 11.2 %copy-start.42 = (f32[2560]{0:T(1024)}, f32[2560]{0:T(1024)S(1)}, u32[]{:S(2)}) copy-start(f32[2560]{0:T(1024)S(1)} %get-tuple-element.21) | copy-start | bytes 30724
  3.7 47.9 %copy-start.44 = (f32[2560]{0:T(1024)}, f32[2560]{0:T(1024)S(1)}, u32[]{:S(2)}) copy-start(f32[2560]{0:T(1024)S(1)} %get-tuple-element.20) | copy-start | bytes 30724
  14.9 2.0 copy-start.5
  20.2 51.5 %copy-start.2 = (f32[256,128]{1,0:T(8,128)}, f32[256,128]{1,0:T(8,128)S(1)}, u32[]{:S(2)}) copy-start(f32[256,128]{1,0:T(8,128)S(1)} %get-tuple-element.63) | copy-start | bytes 393220
  20.3 2.9 copy-start.22
  20.3 2.9 copy-start.25
  21.3 17.8 %collective-permute-start = (bf16[1,128,8,256]{3,1,2,0:T(8,128)(2,1)}, bf16[1,128,8,256]{3,1,2,0:T(8,128)(2,1)}, u32[]{:S(2)}, u32[]{:S(2)}) collective-permute-start(bf16[1,128,8,256]{3,1,2,0:T(8,128)(2,1)} %fusion.146), channel_id=1, source_target_pairs={{0,1},{1,2},{2,3},{3,4},{4,5},{5,6},{6,7},{7,8},{8,9},{9,10},{10,1... | collective-permute-start | bytes 1572872 | tf_op jit(solution)/shard_map/ppermute | solution.py:433
  23.6 18.6 %copy-start.32 = (bf16[1,256,4,256]{1,3,2,0:T(8,128)(2,1)}, bf16[1,256,4,256]{1,3,2,0:T(8,128)(2,1)S(1)}, u32[]{:S(2)}) copy-start(bf16[1,256,4,256]{1,3,2,0:T(8,128)(2,1)S(1)} %copy.125) | copy-start | bytes 1572868
  24.5 17.6 %copy-start.48 = (f32[4,2]{1,0:T(4,128)}, f32[4,2]{1,0:T(4,128)S(1)}, u32[]{:S(2)}) copy-start(f32[4,2]{1,0:T(4,128)S(1)} %max.31) | copy-start | bytes 100
  28.1 2.4 copy-start.19
  38.4 2.3 copy-start.23
  38.4 2.3 copy-start.26
  38.6 3.7 %copy-start.30 = (pred[256,384]{0,1:T(8,128)(4,1)}, pred[256,384]{0,1:T(8,128)(4,1)S(1)}, u32[]{:S(2)}) copy-start(pred[256,384]{0,1:T(8,128)(4,1)S(1)} %compare_and_fusion) | copy-start | bytes 294916
  39.0 2.3 copy-start.15
  39.0 2.3 copy-start.17
  41.4 2.0 copy-start
  41.4 2.0 copy-start.40
  41.5 2.0 copy-start.36
  51.0 10.5 %copy-start.20 = (bf16[1,256,2560]{2,1,0:T(8,128)(2,1)}, bf16[1,256,2560]{2,1,0:T(8,128)(2,1)S(1)}, u32[]{:S(2)}) copy-start(bf16[1,256,2560]{2,1,0:T(8,128)(2,1)S(1)} %get-tuple-element.73) | copy-start | bytes 3932164
  51.6 9.9 %copy-start.57 = (f32[256]{0:T(256)}, f32[256]{0:T(256)S(1)}, u32[]{:S(2)}) copy-start(f32[256]{0:T(256)S(1)} %get-tuple-element.67) | copy-start | bytes 3076
  72.2 2.7 copy-start.14
  216.8 2.0 copy-start.3
  216.8 2.0 copy-start.11
  227.4 2.3 copy-start.45
  227.4 2.3 copy-start.58
  229.6 11.8 %copy-start.56 = (f32[256]{0:T(256)S(1)}, f32[256]{0:T(256)}, u32[]{:S(2)}) copy-start(f32[256]{0:T(256)} %get-tuple-element.66) | copy-start | bytes 3076
  245.8 10.5 %copy-start.1 = (f32[4,384,256,2]{2,1,3,0:T(8,128)S(1)}, f32[4,384,256,2]{2,1,3,0:T(8,128)}, u32[]{:S(2)}) copy-start(f32[4,384,256,2]{2,1,3,0:T(8,128)} %copy-done) | copy-start | bytes 9437188
  245.8 10.5 %copy-start.31 = (pred[256,384]{0,1:T(8,128)(4,1)S(1)}, pred[256,384]{0,1:T(8,128)(4,1)}, u32[]{:S(2)}) copy-start(pred[256,384]{0,1:T(8,128)(4,1)} %copy-done.30) | copy-start | bytes 294916
  245.8 10.5 %copy-start.37 = (f32[4,2,256]{2,1,0:T(2,128)S(1)}, f32[4,2,256]{2,1,0:T(2,128)}, u32[]{:S(2)}) copy-start(f32[4,2,256]{2,1,0:T(2,128)} %copy-done.36) | copy-start | bytes 24580
  245.8 10.5 %copy-start.47 = (f32[4,2,256]{2,1,0:T(2,128)S(1)}, f32[4,2,256]{2,1,0:T(2,128)}, u32[]{:S(2)}) copy-start(f32[4,2,256]{2,1,0:T(2,128)} %copy-done.46) | copy-start | bytes 24580
  256.3 2.8 copy-start.29
  259.1 2.1 copy-start.39
  259.1 2.1 copy-start.41
  259.1 2.1 copy-start.49
  266.0 2.5 copy-start.6
  268.5 10.3 %copy-start.21 = (bf16[1,256,2560]{2,1,0:T(8,128)(2,1)S(1)}, bf16[1,256,2560]{2,1,0:T(8,128)(2,1)}, u32[]{:S(2)}) copy-start(bf16[1,256,2560]{2,1,0:T(8,128)(2,1)} %copy-done.20) | copy-start | bytes 3932164
  268.5 10.3 %copy-start.51 = (f32[2560]{0:T(1024)S(1)}, f32[2560]{0:T(1024)}, u32[]{:S(2)}) copy-start(f32[2560]{0:T(1024)} %get-tuple-element.18) | copy-start | bytes 30724
  268.5 10.3 %copy-start.60 = (bf16[256,2048]{1,0:T(8,128)(2,1)S(1)}, bf16[256,2048]{1,0:T(8,128)(2,1)}, u32[]{:S(2)}) copy-start(bf16[256,2048]{1,0:T(8,128)(2,1)} %get-tuple-element.10) | copy-start | bytes 3145732
  269.8 34.5 %collective-permute-start.1 = (bf16[1,128,8,256]{3,1,2,0:T(8,128)(2,1)}, bf16[1,128,8,256]{3,1,2,0:T(8,128)(2,1)}, u32[]{:S(2)}, u32[]{:S(2)}) collective-permute-start(bf16[1,128,8,256]{3,1,2,0:T(8,128)(2,1)} %get-tuple-element.39), channel_id=1, source_target_pairs={{1,0},{2,1},{3,2},{4,3},{5,4},{6,5},{7,6},{8,7},{9,8},{10,9},{11,1... | collective-permute-start | bytes 1572872 | tf_op jit(solution)/shard_map/ppermute | solution.py:458
  292.4 3.1 copy-start.52
  307.6 4.6 %copy-start.8 = (bf16[1,256,2560]{2,1,0:T(8,128)(2,1)S(1)}, bf16[1,256,2560]{2,1,0:T(8,128)(2,1)}, u32[]{:S(2)}) copy-start(bf16[1,256,2560]{2,1,0:T(8,128)(2,1)} %param.8) | copy-start | bytes 3932164
  307.6 4.6 %copy-start.43 = (f32[2560]{0:T(1024)S(1)}, f32[2560]{0:T(1024)}, u32[]{:S(2)}) copy-start(f32[2560]{0:T(1024)} %copy-done.42) | copy-start | bytes 30724
  307.6 4.6 %copy-start.55 = (f32[256]{0:T(256)S(1)}, f32[256]{0:T(256)}, u32[]{:S(2)}) copy-start(f32[256]{0:T(256)} %copy-done.54) | copy-start | bytes 3076
  312.2 12.2 %copy-start.4 = (f32[1,256,4,2,256]{1,4,3,2,0:T(8,128)S(1)}, f32[1,256,4,2,256]{1,4,3,2,0:T(8,128)}, u32[]{:S(2)}) copy-start(f32[1,256,4,2,256]{1,4,3,2,0:T(8,128)} %copy.156) | copy-start | bytes 6291460
  324.3 3.6 %copy-start.10 = (bf16[1,256,2560]{2,1,0:T(8,128)(2,1)S(1)}, bf16[1,256,2560]{2,1,0:T(8,128)(2,1)}, u32[]{:S(2)}) copy-start(bf16[1,256,2560]{2,1,0:T(8,128)(2,1)} %copy-done.9) | copy-start | bytes 3932164
  324.3 3.6 %copy-start.12 = (f32[256,2560]{1,0:T(8,128)S(1)}, f32[256,2560]{1,0:T(8,128)}, u32[]{:S(2)}) copy-start(f32[256,2560]{1,0:T(8,128)} %get-tuple-element.77) | copy-start | bytes 7864324
  324.3 3.6 %copy-start.53 = (f32[256]{0:T(256)S(1)}, f32[256]{0:T(256)}, u32[]{:S(2)}) copy-start(f32[256]{0:T(256)} %get-tuple-element.64) | copy-start | bytes 3076
  (16 other events, 20.1 us)

commit v2 on v1

--- a/solution.py
+++ b/solution.py
@@ -28,74 +28,6 @@
     inv_freq = (1.0 - ramp_pos) / freq_base + ramp_pos / (YARN_FACTOR * freq_base)
     angles = positions.astype(jnp.float32)[:, None] * inv_freq[None, :]
     return jnp.cos(angles) * concentration, jnp.sin(angles) * concentration
-
-
-def rotate_half(tensor, cos_tab, sin_tab):
-    half_dim = tensor.shape[-1] // 2
-    first_half = tensor[..., :half_dim]
-    second_half = tensor[..., half_dim:]
-    return jnp.concatenate([first_half * cos_tab - second_half * sin_tab, second_half * cos_tab + first_half * sin_tab], axis=-1)
-
-
-def norm_project(hid_f, gain_row, w_in, bias_row, cos_tab, sin_tab, num_heads, kv_heads):
-    batch_size, seq_dev = hid_f.shape[0], hid_f.shape[1]
-    head_dim = 2 * cos_tab.shape[-1]
-    q_width = num_heads * head_dim
-    k_width = kv_heads * head_dim
-    inv_rms = lax.rsqrt(jnp.mean(hid_f * hid_f, axis=-1, keepdims=True) + EPSILON)
-    normed = (hid_f * inv_rms * gain_row).astype(jnp.bfloat16)
-    projected = jnp.dot(normed, w_in, preferred_element_type=jnp.float32) + bias_row
-    query_rows = rotate_half(projected[..., :q_width].reshape(batch_size, seq_dev, kv_heads, num_heads // kv_heads, head_dim), cos_tab[:, None, None, :], sin_tab[:, None, None, :])
-    key_rows = rotate_half(projected[..., q_width:q_width + k_width].reshape(batch_size, seq_dev, kv_heads, head_dim), cos_tab[:, None, :], sin_tab[:, None, :])
-    value_rows = projected[..., q_width + k_width:].reshape(batch_size, seq_dev, kv_heads, head_dim)
-    return query_rows.astype(jnp.bfloat16), key_rows.astype(jnp.bfloat16), value_rows.astype(jnp.bfloat16), inv_rms
-
-
-def attend_forward(query_rows, key_rows, value_rows, sink_row, row_pos, key_pos, window_on, logit_scale):
-    kv_heads, group_size = query_rows.shape[2], query_rows.shape[3]
-    scores = jnp.einsum('bqkgd,bskd->bkgqs', query_rows, key_rows, preferred_element_type=jnp.float32) * logit_scale
-    key_mask = (key_pos[None, :] <= row_pos[:, None]) & (key_pos[None, :] >= 0)
-    if window_on:
-        key_mask = key_mask & (key_pos[None, :] >= row_pos[:, None] - WINDOW)
-    scores = jnp.where(key_mask, scores, -jnp.inf)
-    sink_grid = sink_row.reshape(kv_heads, group_size)[None, :, :, None]
-    row_peak = jnp.maximum(jnp.max(scores, axis=-1), sink_grid)
-    exp_scores = jnp.exp(scores - row_peak[..., None])
-    sink_exp = jnp.exp(sink_grid - row_peak)
-    denominator = jnp.sum(exp_scores, axis=-1) + sink_exp
-    prob_f32 = exp_scores / denominator[..., None]
-    prob_bf = prob_f32.astype(jnp.bfloat16)
-    attn_out = jnp.einsum('bkgqs,bskd->bqkgd', prob_bf, value_rows, preferred_element_type=jnp.float32).astype(jnp.bfloat16)
-    return attn_out, prob_f32, prob_bf, sink_exp / denominator
-
-
-def attend_backward(d_attn, query_rows, key_rows, value_rows, prob_f32, prob_bf, sink_prob, logit_scale):
-    d_prob = jnp.einsum('bqkgd,bskd->bkgqs', d_attn, value_rows, preferred_element_type=jnp.float32).astype(jnp.bfloat16).astype(jnp.float32)
-    row_delta = jnp.sum(prob_f32 * d_prob, axis=-1)
-    d_scores = (prob_f32 * (d_prob - row_delta[..., None])).astype(jnp.bfloat16)
-    d_query = (jnp.einsum('bkgqs,bskd->bqkgd', d_scores, key_rows, preferred_element_type=jnp.float32) * logit_scale).astype(jnp.bfloat16)
-    d_keys = jnp.einsum('bkgqs,bqkgd->bskd', d_scores, query_rows, preferred_element_type=jnp.float32) * logit_scale
-    d_values = jnp.einsum('bkgqs,bqkgd->bskd', prob_bf, d_attn, preferred_element_type=jnp.float32)
-    d_sink = -jnp.sum(sink_prob * row_delta, axis=(0, 3)).reshape(-1)
-    return d_query, d_keys, d_values, d_sink
-
-
-def project_backward(d_query, d_keys, d_values, hid_f, inv_rms, gain_row, w_in, cos_tab, sin_tab):
-    batch_size, seq_dev = hid_f.shape[0], hid_f.shape[1]
-    dq_rot = rotate_half(d_query.astype(jnp.float32), cos_tab[:, None, None, :], -sin_tab[:, None, None, :]).reshape(batch_size, seq_dev, -1)
-    dk_rot = rotate_half(d_keys.astype(jnp.float32), cos_tab[:, None, :], -sin_tab[:, None, :]).reshape(batch_size, seq_dev, -1)
-    d_proj = jnp.concatenate([dq_rot, dk_rot, d_values.astype(jnp.float32).reshape(batch_size, seq_dev, -1)], axis=-1)
-    d_bias = jnp.sum(d_proj, axis=(0, 1))
-    d_normed = jnp.einsum('bsq,dq->bsd', d_proj.astype(jnp.bfloat16), w_in, preferred_element_type=jnp.float32).astype(jnp.bfloat16).astype(jnp.float32)
-    d_gain = jnp.sum(d_normed * hid_f * inv_rms, axis=(0, 1))
-    unit_grad = d_normed * gain_row
-    d_hid = inv_rms * unit_grad - hid_f * inv_rms ** 3 * jnp.mean(unit_grad * hid_f, axis=-1, keepdims=True)
-    return d_hid, d_gain, d_bias
-
-
-def dense_out(attn_out, w_proj, bias_row):
-    batch_size, seq_dev = attn_out.shape[0], attn_out.shape[1]
-    return jnp.dot(attn_out.reshape(batch_size, seq_dev, -1), w_proj, preferred_element_type=jnp.float32) + bias_row
 
 
 MESH = pl.DeviceIdType.MESH
@@ -409,10 +341,339 @@
     )(sinks, q2, kv2, do2)
 
 
+def rotate_tile(tile, cos, sin, width):
+    half = width // 2
+    parts = []
+    for start in range(0, tile.shape[1], width):
+        first, second = tile[:, start:start + half], tile[:, start + half:start + width]
+        parts += [first * cos - second * sin, second * cos + first * sin]
+    return jnp.concatenate(parts, axis=1)
+
+
+def near_mask(shape, me):
+    key_row = lax.broadcasted_iota(jnp.int32, shape, 0)
+    query_row = lax.broadcasted_iota(jnp.int32, shape, 1)
+    first_key = jnp.where(me > 0, 0, WINDOW)
+    return (key_row >= first_key) & (key_row - WINDOW <= query_row) & (key_row >= query_row)
+
+
+def forward_kernel(dims, sink_ref, hid_ref, grad_ref, gain_ref, bqkv_ref, bout_ref, cos_ref, sin_ref, wqkv_hbm, wout_hbm,
+                   q_one, ext_one, lse_one, mid_out, q_two, kv_two, do_two,
+                   ring, wout_one, wout_two, normed, attn, ring_sem, wout_sem, halo_ssem, halo_rsem):
+    kv_heads, num_heads, rows, width, model, num_shards, tile, depth = dims
+    me = lax.axis_index('cp')
+    follow, before = lax.rem(me + 1, num_shards), lax.rem(me + num_shards - 1, num_shards)
+    group = num_heads // kv_heads
+    qw = num_heads * width
+    kw = kv_heads * width
+    q_tiles, k_tiles = qw // tile, kw // tile
+    per_layer = q_tiles + 2 * k_tiles
+    scale = width ** -0.5
+
+    def weight(seq):
+        layer, spot = seq // per_layer, lax.rem(seq, per_layer)
+        col = pl.multiple_of(lax.rem(spot + q_tiles, per_layer) * tile, tile)
+        slot = lax.rem(seq, depth)
+        return pltpu.make_async_copy(wqkv_hbm.at[layer, :, pl.ds(col, tile)], ring.at[slot], ring_sem.at[slot])
+
+    for seq in range(depth):
+        weight(seq).start()
+
+    barrier = pltpu.get_barrier_semaphore()
+    for other in (follow, before):
+        pl.semaphore_signal(barrier, inc=1, device_id={'cp': other}, device_id_type=MESH)
+    pl.semaphore_wait(barrier, 2)
+
+    def normalize(source, layer):
+        hid = source[...].astype(F32)
+        inv = lax.rsqrt(jnp.mean(hid * hid, axis=-1, keepdims=True) + EPSILON)
+        normed[...] = (hid * inv * gain_ref[layer:layer + 1, :]).astype(BF16)
+
+    def project(layer, first, count, rotate, store):
+        def step(i, carry):
+            seq = layer * per_layer + first + i
+            weight(seq).wait()
+            col = pl.multiple_of((first + q_tiles + i) % per_layer * tile, tile)
+            out = jnp.dot(normed[...], ring[lax.rem(seq, depth)], preferred_element_type=F32) + bqkv_ref[layer:layer + 1, pl.ds(col, tile)]
+            if rotate:
+                out = rotate_tile(out, cos_ref[...], sin_ref[...], width)
+            store(i, out.astype(BF16))
+
+            @pl.when(seq + depth < 2 * per_layer)
+            def _():
+                weight(seq + depth).start()
+            return carry
+
+        lax.fori_loop(0, count, step, 0)
+
+    def at(col):
+        return pl.ds(pl.multiple_of(col * tile, tile), tile)
+
+    def halo(i):
+        return pltpu.make_async_remote_copy(src_ref=ext_one.at[pl.ds(rows, WINDOW), at(i)], dst_ref=ext_one.at[pl.ds(0, WINDOW), at(i)],
+                                            send_sem=halo_ssem.at[i], recv_sem=halo_rsem.at[i], device_id={'cp': follow}, device_id_type=MESH)
+
+    def store_near(base):
+        def store(i, out):
+            ext_one[pl.ds(WINDOW, rows), at(base + i)] = out
+            halo(base + i).start()
+        return store
+
+    def store_flat(ref, base):
+        def store(i, out):
+            ref[:, at(base + i)] = out
+        return store
+
+    normalize(hid_ref, 0)
+    project(0, 0, k_tiles, True, store_near(0))
+    project(0, k_tiles, k_tiles, False, store_near(k_tiles))
+    load_two = pltpu.make_async_copy(wout_hbm.at[1], wout_two, wout_sem.at[1])
+    load_two.start()
+    project(0, 2 * k_tiles, q_tiles, True, store_flat(q_one, 0))
+    load_one = pltpu.make_async_copy(wout_hbm.at[0], wout_one, wout_sem.at[0])
+    load_one.start()
+
+    load_two.wait()
+
+    def attn_grad(i, carry):
+        do_two[:, at(i)] = lax.dot_general(grad_ref[...], wout_two[at(i), :], (((1,), (1,)), ((), ())), preferred_element_type=F32).astype(BF16)
+        return carry
+
+    lax.fori_loop(0, q_tiles, attn_grad, 0)
+    for i in range(2 * k_tiles):
+        halo(i).wait_recv()
+
+    def near_head(h, carry):
+        kv = h // group
+        key_cols = pl.ds(pl.multiple_of(kv * width, width), width)
+        value_cols = pl.ds(pl.multiple_of(kw + kv * width, width), width)
+        head_cols = pl.ds(pl.multiple_of(h * width, width), width)
+        logits = lax.dot_general(ext_one[:, key_cols], q_one[:, head_cols], (((1,), (1,)), ((), ())), preferred_element_type=F32) * scale
+        logits = jnp.where(near_mask(logits.shape, me), logits, -jnp.inf)
+        sink = sink_ref[0, h]
+        peak = jnp.maximum(jnp.max(logits, axis=0, keepdims=True), sink)
+        weights = jnp.exp(logits - peak)
+        total = jnp.sum(weights, axis=0, keepdims=True) + jnp.exp(sink - peak)
+        prob = (weights / total).astype(BF16)
+        lse_one[h] = peak + jnp.log(total)
+        attn[:, head_cols] = lax.dot_general(prob, ext_one[:, value_cols], (((0,), (0,)), ((), ())), preferred_element_type=F32).astype(BF16)
+        return carry
+
+    lax.fori_loop(0, num_heads, near_head, 0)
+    load_one.wait()
+
+    def mix(i, carry):
+        out = jnp.dot(attn[...], wout_one[:, at(i)], preferred_element_type=F32)
+        mid_out[:, at(i)] = (hid_ref[:, at(i)].astype(F32) + (out + bout_ref[0:1, at(i)])).astype(BF16)
+        return carry
+
+    lax.fori_loop(0, model // tile, mix, 0)
+    normalize(mid_out, 1)
+    project(1, 0, k_tiles, True, store_flat(kv_two, 0))
+    project(1, k_tiles, k_tiles, False, store_flat(kv_two, k_tiles))
+    project(1, 2 * k_tiles, q_tiles, True, store_flat(q_two, 0))
+    for i in range(2 * k_tiles):
+        halo(i).wait_send()
+
+
+def backward_kernel(dims, sink_ref, o_two, dq_two, dkv_two, hid_ref, mid_ref, grad_ref, q_one, ext_one, lse_one, gain_ref, bout_ref, cos_ref, sin_ref, wqkv_hbm, wout_hbm,
+                    out_ref, d_hid_ref, d_gain_ref, d_bqkv_ref, d_bout_ref, d_sink_ref,
+                    ring, wout_one, wout_two, d_proj, d_norm, d_mid, d_attn, d_own, halo_send, halo_recv, ring_sem, wout_sem, halo_ssem, halo_rsem):
+    kv_heads, num_heads, rows, width, model, num_shards, tile, depth = dims
+    me = lax.axis_index('cp')
+    follow, before = lax.rem(me + 1, num_shards), lax.rem(me + num_shards - 1, num_shards)
+    group = num_heads // kv_heads
+    qw = num_heads * width
+    kw = kv_heads * width
+    tiles = model // tile
+    scale = width ** -0.5
+
+    def weight(seq):
+        layer, spot = 1 - seq // tiles, lax.rem(seq, tiles)
+        slot = lax.rem(seq, depth)
+        return pltpu.make_async_copy(wqkv_hbm.at[layer, pl.ds(pl.multiple_of(spot * tile, tile), tile), :], ring.at[slot], ring_sem.at[slot])
+
+    for seq in range(depth):
+        weight(seq).start()
+    load_one = pltpu.make_async_copy(wout_hbm.at[0], wout_one, wout_sem.at[0])
+    load_two = pltpu.make_async_copy(wout_hbm.at[1], wout_two, wout_sem.at[1])
+
+    barrier = pltpu.get_barrier_semaphore()
+    for other in (follow, before):
+        pl.semaphore_signal(barrier, inc=1, device_id={'cp': other}, device_id_type=MESH)
+    pl.semaphore_wait(barrier, 2)
+
+    def at(col):
+        return pl.ds(pl.multiple_of(col * tile, tile), tile)
+
+    def head_at(h):
+        return pl.ds(pl.multiple_of(h * width, width), width)
+
+    def unrotate(layer, h, grad):
+        out = rotate_tile(grad.astype(F32), cos_ref[...], -sin_ref[...], width)
+        put(layer, h, out)
+
+    def put(layer, h, out):
+        d_bqkv_ref[layer:layer + 1, head_at(h)] = jnp.sum(out, axis=0, keepdims=True)
+        d_proj[:, head_at(h)] = out.astype(BF16)
+
+    def project_back(layer, source, skip_ref, target):
+        def step(i, carry):
+            seq = (1 - layer) * tiles + i
+            weight(seq).wait()
+            out = lax.dot_general(d_proj[...], ring[lax.rem(seq, depth)], (((1,), (1,)), ((), ())), preferred_element_type=F32)
+            d_norm[:, at(i)] = out.astype(BF16)
+
+            @pl.when(seq + depth < 2 * tiles)
+            def _():
+                weight(seq + depth).start()
+            return carry
+
+        lax.fori_loop(0, tiles, step, 0)
+        hid = source[...].astype(F32)
+        inv = lax.rsqrt(jnp.mean(hid * hid, axis=-1, keepdims=True) + EPSILON)
+        grad = d_norm[...].astype(F32)
+        d_gain_ref[layer:layer + 1, :] = jnp.sum(grad * hid * inv, axis=0, keepdims=True)
+        unit = grad * gain_ref[layer:layer + 1, :]
+        d_hid = inv * unit - hid * (inv * inv * inv) * jnp.mean(unit * hid, axis=-1, keepdims=True)
+        skip = skip_ref[...].astype(F32)
+        target[...] = (skip + d_hid).astype(BF16)
+
+    def two_heads(h, carry):
+        unrotate(1, h, dq_two[:, head_at(h)])
+        return carry
+
+    def two_keys(h, carry):
+        unrotate(1, num_heads + h, dkv_two[:, head_at(h)])
+        return carry
+
+    def two_values(h, carry):
+        put(1, num_heads + kv_heads + h, dkv_two[:, head_at(kv_heads + h)].astype(F32))
+        return carry
+
+    lax.fori_loop(0, num_heads, two_heads, 0)
+    lax.fori_loop(0, kv_heads, two_keys, 0)
+    lax.fori_loop(0, kv_heads, two_values, 0)
+    load_one.start()
+    project_back(1, mid_ref, grad_ref, d_mid)
+    load_two.start()
+    d_bout_ref[1:2, :] = jnp.sum(grad_ref[...].astype(F32), axis=0, keepdims=True)
+    d_bout_ref[0:1, :] = jnp.sum(d_mid[...].astype(F32), axis=0, keepdims=True)
+    load_one.wait()
+
+    def attn_grad(i, carry):
+        d_attn[:, at(i)] = lax.dot_general(d_mid[...], wout_one[at(i), :], (((1,), (1,)), ((), ())), preferred_element_type=F32).astype(BF16)
+        return carry
+
+    lax.fori_loop(0, qw // tile, attn_grad, 0)
+
+    def halo(g):
+        return pltpu.make_async_remote_copy(src_ref=halo_send.at[g], dst_ref=halo_recv.at[g], send_sem=halo_ssem.at[g], recv_sem=halo_rsem.at[g],
+                                            device_id={'cp': before}, device_id_type=MESH)
+
+    def near_group(g, carry):
+        key_blk, value_blk = ext_one[:, head_at(g)], ext_one[:, head_at(kv_heads + g)]
+        d_key = d_value = None
+        for part in range(group):
+            h = g * group + part
+            query_blk, grad_blk = q_one[:, head_at(h)], d_attn[:, head_at(h)]
+            logits = lax.dot_general(key_blk, query_blk, (((1,), (1,)), ((), ())), preferred_element_type=F32) * scale
+            logits = jnp.where(near_mask(logits.shape, me), logits, -jnp.inf)
+            lse = lse_one[h]
+            prob = jnp.exp(logits - lse)
+            d_prob = lax.dot_general(value_blk, grad_blk, (((1,), (1,)), ((), ())), preferred_element_type=F32).astype(BF16).astype(F32)
+            delta = jnp.sum(prob * d_prob, axis=0, keepdims=True)
+            d_score = (prob * (d_prob - delta)).astype(BF16)
+            d_query = lax.dot_general(d_score, key_blk, (((0,), (0,)), ((), ())), preferred_element_type=F32) * scale
+            unrotate(0, h, d_query.astype(BF16))
+            d_sink = -jnp.sum(jnp.exp(sink_ref[0, h] - lse) * delta, axis=1, keepdims=True)
+            d_sink_ref[h] = jnp.zeros(d_sink_ref.shape[1:], F32) + d_sink
+            one_key = jnp.dot(d_score, query_blk, preferred_element_type=F32)
+            one_value = jnp.dot(prob.astype(BF16), grad_blk, preferred_element_type=F32)
+            d_key = one_key if d_key is None else d_key + one_key
+            d_value = one_value if d_value is None else d_value + one_value
+        d_key = d_key * scale
+        halo_send[g, 0] = d_key[:WINDOW].astype(BF16)
+        halo_send[g, 1] = d_value[:WINDOW].astype(BF16)
+        d_own[0, g] = d_key[WINDOW:]
+        d_own[1, g] = d_value[WINDOW:]
+        halo(g).start()
+        return carry
+
+    lax.fori_loop(0, kv_heads, near_group, 0)
+    load_two.wait()
+
+    def mix(i, carry):
+        out = jnp.dot(o_two[...], wout_two[:, at(i)], preferred_element_type=F32)
+        out_ref[:, at(i)] = (mid_ref[:, at(i)].astype(F32) + (out + bout_ref[1:2, at(i)])).astype(BF16)
+        return carry
+
+    lax.fori_loop(0, tiles, mix, 0)
+    for g in range(kv_heads):
+        halo(g).wait_recv()
+    tail = pl.ds(rows - WINDOW, WINDOW)
+
+    def near_finish(g, carry):
+        for kind in range(2):
+            d_own[kind, g, tail] += halo_recv[g, kind].astype(F32)
+        unrotate(0, num_heads + g, d_own[0, g].astype(BF16))
+        put(0, num_heads + kv_heads + g, d_own[1, g].astype(BF16).astype(F32))
+        return carry
+
+    lax.fori_loop(0, kv_heads, near_finish, 0)
+    project_back(0, hid_ref, d_mid, d_hid_ref)
+    for g in range(kv_heads):
+        halo(g).wait_send()
+
+
+def forward_call(hid, grad, gain, bqkv, bout, cos, sin, wqkv, wout, sinks, kv_heads, num_shards):
+    rows, model = hid.shape
+    num_heads = sinks.shape[1]
+    width = wout.shape[1] // num_heads
+    qw, kw = num_heads * width, kv_heads * width
+    tile, depth = 512, 4
+    vm, dma = pltpu.VMEM, pltpu.SemaphoreType.DMA
+    space, far = pl.BlockSpec(memory_space=pltpu.VMEM), pl.BlockSpec(memory_space=pl.ANY)
+    shape = jax.ShapeDtypeStruct
+    return pl.pallas_call(
+        functools.partial(forward_kernel, (kv_heads, num_heads, rows, width, model, num_shards, tile, depth)),
+        out_shape=[shape((rows, qw), BF16), shape((WINDOW + rows, 2 * kw), BF16), shape((num_heads, 1, rows), F32), shape((rows, model), BF16),
+                   shape((rows, qw), BF16), shape((rows, 2 * kw), BF16), shape((rows, qw), BF16)],
+        in_specs=[pl.BlockSpec(memory_space=pltpu.SMEM)] + [space] * 7 + [far] * 2,
+        out_specs=[space] * 7,
+        scratch_shapes=[vm((depth, model, tile), BF16), vm((qw, model), BF16), vm((qw, model), BF16), vm((rows, model), BF16), vm((rows, qw), BF16),
+                        dma((depth,)), dma((2,)), dma((2 * kw // tile,)), dma((2 * kw // tile,))],
+        compiler_params=pltpu.CompilerParams(collective_id=1, has_side_effects=True, vmem_limit_bytes=67043328),
+        name='forward_dense',
+    )(sinks, hid, grad, gain, bqkv, bout, cos, sin, wqkv, wout)
+
+
+def backward_call(o_two, dq_two, dkv_two, hid, mid, grad, q_one, ext_one, lse_one, gain, bout, cos, sin, wqkv, wout, sinks, kv_heads, num_shards):
+    rows, model = hid.shape
+    num_heads = sinks.shape[1]
+    width = wout.shape[1] // num_heads
+    qw, kw = num_heads * width, kv_heads * width
+    tile, depth = 512, 3
+    vm, dma = pltpu.VMEM, pltpu.SemaphoreType.DMA
+    space, far = pl.BlockSpec(memory_space=pltpu.VMEM), pl.BlockSpec(memory_space=pl.ANY)
+    shape = jax.ShapeDtypeStruct
+    return pl.pallas_call(
+        functools.partial(backward_kernel, (kv_heads, num_heads, rows, width, model, num_shards, tile, depth)),
+        out_shape=[shape((rows, model), BF16), shape((rows, model), BF16), shape((2, model), F32), shape((2, qw + 2 * kw), F32), shape((2, model), F32),
+                   shape((num_heads, 8, 128), F32)],
+        in_specs=[pl.BlockSpec(memory_space=pltpu.SMEM)] + [space] * 13 + [far] * 2,
+        out_specs=[space] * 6,
+        scratch_shapes=[vm((depth, tile, qw + 2 * kw), BF16), vm((qw, model), BF16), vm((qw, model), BF16), vm((rows, qw + 2 * kw), BF16), vm((rows, model), BF16),
+                        vm((rows, model), BF16), vm((rows, qw), BF16), vm((2, kv_heads, rows, width), F32),
+                        vm((kv_heads, 2, WINDOW, width), BF16), vm((kv_heads, 2, WINDOW, width), BF16),
+                        dma((depth,)), dma((2,)), dma((kv_heads,)), dma((kv_heads,))],
+        compiler_params=pltpu.CompilerParams(collective_id=2, has_side_effects=True, vmem_limit_bytes=67043328),
+        name='backward_dense',
+    )(sinks, o_two, dq_two, dkv_two, hid, mid, grad, q_one, ext_one, lse_one, gain, bout, cos, sin, wqkv, wout)
+
+
 def solution(mesh):
     num_shards = mesh.shape['cp']
-    forward_pairs = [(source, source + 1) for source in range(num_shards - 1)]
-    backward_pairs = [(source + 1, source) for source in range(num_shards - 1)]
     row_spec = P('dp', 'cp')
     device_spec = P(('dp', 'cp'))
     whole_spec = P()
@@ -422,50 +683,16 @@
         num_heads = attn_sinks.shape[1]
         head_dim = w_out.shape[1] // num_heads
         kv_heads = (w_qkv.shape[2] // head_dim - num_heads) // 2
-        logit_scale = head_dim ** -0.5
-        shard_start = lax.axis_index('cp') * seq_dev
-        row_pos = shard_start + jnp.arange(seq_dev)
+        row_pos = lax.axis_index('cp') * seq_dev + jnp.arange(seq_dev)
         cos_tab, sin_tab = rope_tables(row_pos, head_dim)
-
-        hid_one = hidden.astype(jnp.float32)
-        query_one, keys_one, values_one, rms_one = norm_project(hid_one, norm_gain[0], w_qkv[0], b_qkv[0], cos_tab, sin_tab, num_heads, kv_heads)
-        tail_rows = jnp.concatenate([keys_one[:, seq_dev - WINDOW:], values_one[:, seq_dev - WINDOW:]], axis=2)
-        prev_rows = lax.ppermute(tail_rows, 'cp', forward_pairs)
-        near_keys = jnp.concatenate([prev_rows[:, :, :kv_heads], keys_one], axis=1)
-        near_values = jnp.concatenate([prev_rows[:, :, kv_heads:], values_one], axis=1)
-        near_pos = jnp.concatenate([shard_start - WINDOW + jnp.arange(WINDOW), row_pos])
-        attn_one, prob_one, probbf_one, sink_one = attend_forward(query_one, near_keys, near_values, attn_sinks[0], row_pos, near_pos, True, logit_scale)
-        middle = (hid_one + dense_out(attn_one, w_out[0], b_out[0])).astype(jnp.bfloat16)
-
-        hid_two = middle.astype(jnp.float32)
-        query_two, keys_two, values_two, rms_two = norm_project(hid_two, norm_gain[1], w_qkv[1], b_qkv[1], cos_tab, sin_tab, num_heads, kv_heads)
-        d_out_two = grad_out.astype(jnp.float32)
-        d_attn_two = jnp.einsum('bsd,qd->bsq', grad_out, w_out[1], preferred_element_type=jnp.float32).astype(jnp.bfloat16)
-        flat_two = jnp.concatenate([keys_two.reshape(seq_dev, -1), values_two.reshape(seq_dev, -1)], axis=1)
-        attn_two, dq_two, own_two, dsink_wide = far_attention(query_two.reshape(seq_dev, -1), flat_two, d_attn_two.reshape(seq_dev, -1), attn_sinks[1], kv_heads, num_shards)
-        attn_two = attn_two.reshape(1, seq_dev, -1)
-        dq_two = dq_two.reshape(query_two.shape)
-        own_two = own_two.reshape(1, seq_dev, 2 * kv_heads, head_dim)
-        dsink_two = dsink_wide[:, 0, 0]
-        output = (hid_two + dense_out(attn_two, w_out[1], b_out[1])).astype(jnp.bfloat16)
-        dhid_two, dgain_two, dbias_two = project_backward(dq_two, own_two[:, :, :kv_heads], own_two[:, :, kv_heads:], hid_two, rms_two, norm_gain[1], w_qkv[1], cos_tab, sin_tab)
-        d_middle = (d_out_two + dhid_two).astype(jnp.bfloat16)
-
-        d_mid_f = d_middle.astype(jnp.float32)
-        d_attn_one = jnp.einsum('bsd,qd->bsq', d_middle, w_out[0], preferred_element_type=jnp.float32).astype(jnp.bfloat16).reshape(query_one.shape)
-        dq_one, dk_near, dv_near, dsink_one = attend_backward(d_attn_one, query_one, near_keys, near_values, prob_one, probbf_one, sink_one, logit_scale)
-        near_grad = jnp.concatenate([dk_near, dv_near], axis=2)
-        prev_grad = lax.ppermute(near_grad[:, :WINDOW].astype(jnp.bfloat16), 'cp', backward_pairs)
-        own_grad = near_grad[:, WINDOW:]
-        cut_row = seq_dev - WINDOW
-        own_one = jnp.concatenate([own_grad[:, :cut_row], own_grad[:, cut_row:] + prev_grad.astype(jnp.float32)], axis=1).astype(jnp.bfloat16)
-        dhid_one, dgain_one, dbias_one = project_backward(dq_one, own_one[:, :, :kv_heads], own_one[:, :, kv_heads:], hid_one, rms_one, norm_gain[0], w_qkv[0], cos_tab, sin_tab)
-        d_hidden = (d_mid_f + dhid_one).astype(jnp.bfloat16)
-
-        d_gain = jnp.stack([dgain_one, dgain_two])[None]
-        d_bias_qkv = jnp.stack([dbias_one, dbias_two])[None]
-        d_bias_out = jnp.stack([jnp.sum(d_mid_f, axis=(0, 1)), jnp.sum(d_out_two, axis=(0, 1))])[None]
-        d_sinks = jnp.stack([dsink_one, dsink_two])[None]
-        return output, d_hidden, d_gain, d_bias_qkv, d_bias_out, d_sinks
+        hid, grad = hidden[0], grad_out[0]
+
+        query_one, near_one, lse_one, middle, query_two, flat_two, d_attn_two = forward_call(
+            hid, grad, norm_gain, b_qkv, b_out, cos_tab, sin_tab, w_qkv, w_out, attn_sinks, kv_heads, num_shards)
+        attn_two, dq_two, dkv_two, dsink_two = far_attention(query_two, flat_two, d_attn_two, attn_sinks[1], kv_heads, num_shards)
+        output, d_hidden, d_gain, d_bias_qkv, d_bias_out, dsink_one = backward_call(
+            attn_two, dq_two, dkv_two, hid, middle, grad, query_one, near_one, lse_one, norm_gain, b_out, cos_tab, sin_tab, w_qkv, w_out, attn_sinks, kv_heads, num_shards)
+        d_sinks = jnp.stack([dsink_one[:, 0, 0], dsink_two[:, 0, 0]])
+        return output[None], d_hidden[None], d_gain[None], d_bias_qkv[None], d_bias_out[None], d_sinks[None]
 
     return jax.shard_map(local_step, mesh=mesh, in_specs=(row_spec, row_spec, whole_spec, whole_spec, whole_spec, whole_spec, whole_spec, whole_spec), out_specs=(row_spec, row_spec, device_spec, device_spec, device_spec, device_spec), check_vma=False)

time: 336 us -> 236 us (0.70)
  the two profiles are of different devices: /device:TPU:104 before, /device:TPU:97 now
where the time goes in v2:
time: 236 us; the launch traced here: 235 us
  Pallas kernels  224 us (95%)
  local copies, waits for them, and re-layouts  8.46 us (4%)
    pallas_call x1, Pallas kernels, far_attention(): pl.pallas_call(functools.partial(far_attention_kernel, (kv_heads, cores,...  143 us
    pallas_call x1, Pallas kernels, backward_call(): pl.pallas_call(functools.partial(backward_kernel, (kv_heads, num_heads, r...  44.9 us
    pallas_call x1, Pallas kernels, forward_call(): pl.pallas_call(functools.partial(forward_kernel, (kv_heads, num_heads, ro...  36.4 us
    unnamed x13, local copies, waits for them, and re-layouts  5.46 us

profile of v2, /device:TPU:97, one launch (start us, length us, event | category | flops | bytes accessed | tf_op | source)
XLA Modules:
  0.0 235.3 jit_solution(10247120982232937873)
XLA Ops:
  0.6 1.2 slice_bitcast_fusion.sink_ref
  1.8 1.3 fusion.1
  3.1 36.4 %forward_dense.1 = (bf16[256,2048]{1,0:T(8,128)(2,1)}, bf16[384,2048]{1,0:T(8,128)(2,1)}, f32[8,1,256]{2,1,0:T(1,128)}, bf16[256,2560]{1,0:T(8,128)(2,1)}, bf16[...) custom-call(f32[2,8]{1,0:T(2,128)} %sink_ref.3, bf16[256,2560]{1,0:T(8,128)(2,1)} %bitcast.13, ...), custom_call_target="tpu_custom_call" | custom-call | tf_op jit(solution)/shard_map/forward_dense/pallas_call | solution.py:638
  39.6 143.1 %far_attention.1 = (bf16[256,2048]{1,0:T(8,128)(2,1)}, bf16[256,2048]{1,0:T(8,128)(2,1)}, bf16[256,2048]{1,0:T(8,128)(2,1)}, f32[8,8,128]{2,1,0:T(8,128)}) custom-call(f32[8]{0:T(128)} %slice_bitcast_fusion.sink_ref, bf16[256,2048]{1,0:T(8,128)(2,1)} %get-tuple-element.23.q_ref, bf16[256,2048]{1,0:T(8,128)(2,1)} %get-tuple-element.24.kv_ref, ...), custom_call_target="tpu_custom_call" | custom-call | tf_op jit(solution)/shard_map/far_attention/pallas_call | solution.py:332
  182.6 44.9 %backward_dense.1 = (bf16[256,2560]{1,0:T(8,128)(2,1)}, bf16[256,2560]{1,0:T(8,128)(2,1)}, f32[2,2560]{1,0:T(2,128)}, f32[2,4096]{1,0:T(2,128)}, f32[2,2560]{1,0:T(2,128)}, /*index=5*/f32[8,8,128]{2,1,0:T(8,128)}) custom-call(f32[2,8]{1,0:T(2,128)} %sink_ref.3, bf16[256,2048]{1,0:T(8,128)(2,1)} %get-tuple-element.26.o_two, ...), custom_call_target="tpu_custom_call" | custom-call | tf_op jit(solution)/shard_map/backward_dense/pallas_call | solution.py:660
  227.5 0.9 slice_reduce_fusion.1
  228.4 0.9 slice_reduce_fusion
  229.3 0.6 maximum_bitcast_fusion
  229.9 0.0 copy-start
  229.9 2.6 %copy.19 = bf16[1,256,2560]{2,1,0:T(8,128)(2,1)} copy(bf16[1,256,2560]{2,1,0:T(8,128)(2,1)} %bitcast.18) | data formatting | bytes 2621440
  232.4 0.0 copy-done
  232.4 0.0 copy-start.3
  232.4 0.0 copy-start.1
  232.4 0.0 copy-start.2
  232.4 1.1 copy.20
  233.5 0.0 copy-done.3
  233.5 0.6 copy.21
  234.1 0.0 copy-done.1
  234.1 0.6 copy.22
  234.7 0.0 copy-done.2
  234.7 0.6 copy.23
  (2 shorter events, 0.0 us)
Async XLA Ops:
  229.9 2.6 %copy-start = (bf16[256,2560]{1,0:T(8,128)(2,1)S(1)}, bf16[256,2560]{1,0:T(8,128)(2,1)}, u32[]{:S(2)}) copy-start(bf16[256,2560]{1,0:T(8,128)(2,1)} %get-tuple-element.34) | copy-start | bytes 3932164
  232.4 1.1 copy-start.3
  232.4 1.7 copy-start.1
  232.4 2.3 copy-start.2
